TPU v7x, 128 devices: a whole 4x4x4 slice. The times are simulated.
128 devices in a mesh: batch: 1, time: 2 (over core), region: 64 (over z, y, x).
Axes of the slice: x: 4, y: 4, z: 4, core: 2. Of those that a mesh axis runs over, the one named last changes fastest.
Arguments:
- patches: bfloat16 [24576, 1536], P(('batch', 'time', 'region'))
- enc_pos: bfloat16 [24576, 768], P(('batch', 'time', 'region'))
- vis_mask: int32 [24576], P(('batch', 'time', 'region'))
- dec_pos: bfloat16 [24576, 384], P(('batch', 'time', 'region'))
- w_embed: bfloat16 [1536, 768], replicated
- b_embed: float32 [768], replicated
- enc_vec: float32 [2, 12, 768], replicated
- enc_wqkv: bfloat16 [2, 768, 3, 12, 64], replicated
- enc_wo: bfloat16 [2, 12, 64, 768], replicated
- enc_w1: bfloat16 [2, 768, 3072], replicated
- enc_w2: bfloat16 [2, 3072, 768], replicated
- enc_final: float32 [2, 768], replicated
- w_dec_in: bfloat16 [768, 384], replicated
- mask_token: bfloat16 [384], replicated
- dec_vec: float32 [2, 12, 384], replicated
- dec_wqkv: bfloat16 [2, 384, 3, 6, 64], replicated
- dec_wo: bfloat16 [2, 6, 64, 384], replicated
- dec_w1: bfloat16 [2, 384, 1536], replicated
- dec_w2: bfloat16 [2, 1536, 384], replicated
- dec_final: float32 [2, 384], replicated
- w_out: bfloat16 [384, 1536], replicated
Outputs:
- output: float32 [24576, 1536], P(('batch', 'time', 'region'))
All inputs are finite; a program needn't handle non-finite values.
Results may differ from a plain program's by a relative error of at most 0.0143243.
Values are sent between devices in bfloat16 or wider.
A program may use at most 1 GiB of HBM per device.

v0:
```python
import functools
import jax
import jax.numpy as jnp
from jax import lax
from jax.sharding import PartitionSpec as P

KEEP_DIV = 8
LN_EPS = 1e-6
GROUP_AXES = ("time", "region")
TOKEN_AXES = ("batch", "time", "region")


def layer_norm(hidden, ln_gain, ln_shift):
    hid_f32 = hidden.astype(jnp.float32)
    mean_val = jnp.mean(hid_f32, axis=-1, keepdims=True)
    centered = hid_f32 - mean_val
    variance = jnp.mean(centered * centered, axis=-1, keepdims=True)
    return centered * lax.rsqrt(variance + LN_EPS) * ln_gain + ln_shift


def attend(query_rows, key_rows, value_rows, key_bias):
    head_dim = query_rows.shape[-1]
    scores = jnp.einsum("qhd,khd->hqk", query_rows, key_rows, preferred_element_type=jnp.float32) * (head_dim ** -0.5)
    if key_bias is not None:
        scores = scores + key_bias
    attn_probs = jax.nn.softmax(scores, axis=-1).astype(jnp.bfloat16)
    return jnp.einsum("hqk,khd->qhd", attn_probs, value_rows, preferred_element_type=jnp.float32).astype(jnp.bfloat16)


def run_block(hidden, vec_rows, w_qkv, w_o, w_one, w_two, gather_rows, key_bias):
    head_count, head_dim = w_qkv.shape[2], w_qkv.shape[3]
    normed = layer_norm(hidden, vec_rows[0], vec_rows[1]).astype(jnp.bfloat16)
    qkv_bias = jnp.stack([vec_rows[4], jnp.zeros_like(vec_rows[4]), vec_rows[5]]).reshape(1, 3, head_count, head_dim)
    qkv_rows = (jnp.einsum("nd,dche->nche", normed, w_qkv, preferred_element_type=jnp.float32) + qkv_bias).astype(jnp.bfloat16)
    key_rows = gather_rows(qkv_rows[:, 1])
    value_rows = gather_rows(qkv_rows[:, 2])
    attended = attend(qkv_rows[:, 0], key_rows, value_rows, key_bias)
    residual = (hidden.astype(jnp.float32) + jnp.einsum("nhe,hed->nd", attended, w_o, preferred_element_type=jnp.float32) + vec_rows[6]).astype(jnp.bfloat16)
    normed_mlp = layer_norm(residual, vec_rows[2], vec_rows[3]).astype(jnp.bfloat16)
    mlp_hidden = jax.nn.gelu(jnp.dot(normed_mlp, w_one, preferred_element_type=jnp.float32) + vec_rows[8:12].reshape(-1), approximate=False).astype(jnp.bfloat16)
    return (residual.astype(jnp.float32) + jnp.dot(mlp_hidden, w_two, preferred_element_type=jnp.float32) + vec_rows[7]).astype(jnp.bfloat16)


def solution(mesh):
    regions = mesh.shape["region"]
    skew_factor = min(4, regions)
    gather_group = functools.partial(lax.all_gather, axis_name=GROUP_AXES, axis=0, tiled=True)

    def local_step(patches, enc_pos, vis_mask, dec_pos, w_embed, b_embed, enc_vec, enc_wqkv, enc_wo, enc_w1, enc_w2, enc_final, w_dec_in, mask_token, dec_vec, dec_wqkv, dec_wo, dec_w1, dec_w2, dec_final, w_out):
        tokens_dev = patches.shape[0]
        vis_dev = tokens_dev // KEEP_DIV
        cap_rows = skew_factor * vis_dev
        enc_width = w_embed.shape[1]
        dec_width = w_dec_in.shape[1]
        region_pos = lax.axis_index("region")
        own_count = jnp.sum(vis_mask)
        counts = lax.all_gather(own_count[None], "region", axis=0, tiled=True)
        starts = jnp.cumsum(counts) - counts
        offset = starts[region_pos]
        slot_ids = jnp.arange(cap_rows, dtype=jnp.int32)
        local_rank = jnp.cumsum(vis_mask) - 1
        selector = ((local_rank[None, :] == slot_ids[:, None]) & (vis_mask[None, :] == 1)).astype(jnp.bfloat16)
        picked_patch = jnp.dot(selector, patches, preferred_element_type=jnp.float32).astype(jnp.bfloat16)
        picked_pos = jnp.dot(selector, enc_pos, preferred_element_type=jnp.float32)
        embedded = jnp.dot(picked_patch, w_embed, preferred_element_type=jnp.float32) + b_embed + picked_pos
        embedded = jnp.where((slot_ids < own_count)[:, None], embedded, 0.0).astype(jnp.bfloat16)
        rank_space = lax.dynamic_update_slice(jnp.zeros((regions * vis_dev + cap_rows, enc_width), jnp.bfloat16), embedded, (offset, 0))
        send_rows = rank_space[: regions * vis_dev].reshape(regions, vis_dev, enc_width)
        received = lax.all_to_all(send_rows, "region", 0, 0, tiled=True)
        hidden = jnp.sum(received, axis=0)
        for layer_idx in range(enc_vec.shape[0]):
            hidden = run_block(hidden, enc_vec[layer_idx], enc_wqkv[layer_idx], enc_wo[layer_idx], enc_w1[layer_idx], enc_w2[layer_idx], gather_group, None)
        latent = jnp.dot(layer_norm(hidden, enc_final[0], enc_final[1]).astype(jnp.bfloat16), w_dec_in, preferred_element_type=jnp.float32).astype(jnp.bfloat16)
        my_ranks = region_pos * vis_dev + jnp.arange(vis_dev, dtype=jnp.int32)
        from_source = (my_ranks[None, :] >= starts[:, None]) & (my_ranks[None, :] < (starts + counts)[:, None])
        back_rows = jnp.where(from_source[:, :, None], latent[None], jnp.zeros((), jnp.bfloat16))
        returned = lax.all_to_all(back_rows, "region", 0, 0, tiled=True)
        return_space = jnp.concatenate([returned.reshape(regions * vis_dev, dec_width), jnp.zeros((cap_rows, dec_width), jnp.bfloat16)], axis=0)
        own_latent = lax.dynamic_slice(return_space, (offset, 0), (cap_rows, dec_width))
        placed = jnp.einsum("ct,cd->td", selector, own_latent, preferred_element_type=jnp.float32)
        hidden = (jnp.where(vis_mask[:, None] == 1, placed, mask_token.astype(jnp.float32)) + dec_pos.astype(jnp.float32)).astype(jnp.bfloat16)
        for layer_idx in range(dec_vec.shape[0]):
            hidden = run_block(hidden, dec_vec[layer_idx], dec_wqkv[layer_idx], dec_wo[layer_idx], dec_w1[layer_idx], dec_w2[layer_idx], gather_group, None)
        return jnp.dot(layer_norm(hidden, dec_final[0], dec_final[1]).astype(jnp.bfloat16), w_out, preferred_element_type=jnp.float32)

    token_rows = P(TOKEN_AXES, None)
    token_flags = P(TOKEN_AXES)
    replicated = P()
    in_specs = (token_rows, token_rows, token_flags, token_rows) + (replicated,) * 17
    return jax.shard_map(local_step, mesh=mesh, in_specs=in_specs, out_specs=token_rows, check_vma=False)
```

profile of v0, /device:TPU:1, one launch (start us, length us, event | category | flops | bytes accessed | tf_op | source)
XLA Modules:
  0.0 1197.5 jit_solution(7110991718923491970)
XLA Ops:
  12.8 20.9 %all-reduce.2 = s32[64]{0:T(128)S(1)} all-reduce(s32[64]{0:T(128)S(1)} %dynamic-update-slice), channel_id=1, replica_groups=mesh['batch'=1,'time'=2,'region'=64] {'region'}, use_global_device_ids=true, to_apply=%add.2 | all-reduce | flops 64 | bytes 512
  45.8 4.8 all-to-all-start
  51.3 30.3 %all-to-all-done = bf16[64,24,768]{2,1,0:T(8,128)(2,1)S(1)} async-done(((bf16[64,24,768]{2,1,0:T(8,128)(2,1)}), bf16[64,24,768]{2,1,0:T(8,128)(2,1)S(1)}, u32[]{:S(2)}, u32[]{:S(2)}) %all-to-all-start) | async-done | bytes 2359328 | tf_op jit(solution)/shard_map/all_to_all | solution.py:69
  87.4 78.0 %all-gather.19.cloned.1.call-done = bf16[3072,1,12,64]{3,0,2,1:T(8,128)(2,1)} async-done(((bf16[24,1,12,64]{3,0,2,1:T(8,128)(2,1)}), bf16[3072,1,12,64]{3,0,2,1:T(8,128)(2,1)}) %all-gather.19.cloned.1.call-update) | async-done | bytes 4718608 | tf_op jit(solution)/shard_map/all_gather | solution.py:35
  165.3 8.2 fusion.601
  173.5 67.4 %all-gather.17.cloned.1.call-done = bf16[3072,1,12,64]{3,0,2,1:T(8,128)(2,1)} async-done(((bf16[24,1,12,64]{3,0,2,1:T(8,128)(2,1)}), bf16[3072,1,12,64]{3,0,2,1:T(8,128)(2,1)}) %all-gather.17.cloned.1.call-update) | async-done | bytes 4718608 | tf_op jit(solution)/shard_map/all_gather | solution.py:36
  240.9 7.0 fusion.602
  248.1 5.8 fusion.605
  254.1 3.5 fusion.62
  259.2 72.0 %all-gather.23.cloned.1.call-done = bf16[3072,1,12,64]{3,0,2,1:T(8,128)(2,1)} async-done(((bf16[24,1,12,64]{3,0,2,1:T(8,128)(2,1)}), bf16[3072,1,12,64]{3,0,2,1:T(8,128)(2,1)}) %all-gather.23.cloned.1.call-update) | async-done | bytes 4718608 | tf_op jit(solution)/shard_map/all_gather | solution.py:35
  331.2 8.2 fusion.608
  339.4 67.2 %all-gather.21.cloned.1.call-done = bf16[3072,1,12,64]{3,0,2,1:T(8,128)(2,1)} async-done(((bf16[24,1,12,64]{3,0,2,1:T(8,128)(2,1)}), bf16[3072,1,12,64]{3,0,2,1:T(8,128)(2,1)}) %all-gather.21.cloned.1.call-update) | async-done | bytes 4718608 | tf_op jit(solution)/shard_map/all_gather | solution.py:36
  406.7 7.0 fusion.609
  413.9 5.8 fusion.612
  421.5 7.0 all-to-all-start.1
  432.9 15.0 %all-to-all-done.1 = bf16[64,24,384]{2,1,0:T(8,128)(2,1)S(1)} async-done(((bf16[64,24,384]{2,1,0:T(8,128)(2,1)}), bf16[64,24,384]{2,1,0:T(8,128)(2,1)S(1)}, u32[]{:S(2)}, u32[]{:S(2)}) %all-to-all-start.1) | async-done | bytes 1179680 | tf_op jit(solution)/shard_map/all_to_all | solution.py:77
  453.0 129.7 %all-gather.27.cloned.1.call-done = bf16[24576,1,6,64]{3,2,1,0:T(8,128)(2,1)} async-done(((bf16[192,1,6,64]{3,2,1,0:T(8,128)(2,1)}), bf16[24576,1,6,64]{3,2,1,0:T(8,128)(2,1)}) %all-gather.27.cloned.1.call-update) | async-done | bytes 18874384 | tf_op jit(solution)/shard_map/all_gather | solution.py:35
  582.7 48.7 %copy.50 = bf16[24576,1,6,64]{0,3,2,1:T(8,128)(2,1)} copy(bf16[24576,1,6,64]{3,2,1,0:T(8,128)(2,1)} %all-gather.27.cloned.1.call-done) | data formatting | bytes 37748736 | tf_op jit(solution)/shard_map/all_gather | solution.py:35
  631.4 44.8 %multiply_reduce_fusion.1 = (f32[6,192]{1,0:T(8,128)S(1)}, f32[6,192,24576]{2,1,0:T(8,128)}) fusion(bf16[24576,1,6,64]{0,3,2,1:T(8,128)(2,1)} %copy.50, bf16[192,3,6,64]{0,3,2,1:T(8,128)(2,1)S(1)} %add_convert_fusion.1), kind=kOutput, calls=%fused_computation.7 | convolution fusion | flops 3680500736 | bytes 132321792 | tf_op jit(solution)/shard_map/qhd,khd->hqk/dot_general | solution.py:23
  676.2 34.9 %fusion.2 = f32[6,192]{1,0:T(8,128)S(1)} fusion(f32[6,192,24576]{2,1,0:T(8,128)} %get-tuple-element.74, f32[6,192]{1,0:T(8,128)S(1)} %get-tuple-element.73), kind=kLoop, calls=%fused_computation.8 | loop fusion | flops 84933504 | bytes 113255424 | tf_op jit(solution)/shard_map/reduce_sum | solution.py:26
  711.1 8.0 all-gather.25.cloned.1.call-done
  719.1 48.7 %copy.48 = bf16[24576,1,6,64]{0,3,2,1:T(8,128)(2,1)} copy(bf16[24576,1,6,64]{3,2,1,0:T(8,128)(2,1)} %all-gather.25.cloned.1.call-done) | data formatting | bytes 37748736 | tf_op jit(solution)/shard_map/all_gather | solution.py:36
  767.8 43.3 %fusion.153 = bf16[192,6,64]{0,2,1:T(8,128)(2,1)S(1)} fusion(f32[6,192,24576]{2,1,0:T(8,128)} %get-tuple-element.74, f32[6,192]{1,0:T(8,128)S(1)} %fusion.2, f32[6,192]{1,0:T(8,128)S(1)} %get-tuple-element.73, bf16[24576,1,6,64]{0,3,2,1:T(8,128)(2,1)} %copy.48), kind=kOutput, calls=%fused_computation.150 | convolution fusion | flops 3737198592 | bytes 132277248 | tf_op jit(solution)/shard_map/hqk,khd->qhd/dot_general | solution.py:27
  811.9 5.0 fusion.617
  821.4 131.3 %all-gather.31.cloned.1.call-done = bf16[24576,1,6,64]{3,2,1,0:T(8,128)(2,1)} async-done(((bf16[192,1,6,64]{3,2,1,0:T(8,128)(2,1)}), bf16[24576,1,6,64]{3,2,1,0:T(8,128)(2,1)}) %all-gather.31.cloned.1.call-update) | async-done | bytes 18874384 | tf_op jit(solution)/shard_map/all_gather | solution.py:35
  952.7 48.8 %copy.54 = bf16[24576,1,6,64]{0,3,2,1:T(8,128)(2,1)} copy(bf16[24576,1,6,64]{3,2,1,0:T(8,128)(2,1)} %all-gather.31.cloned.1.call-done) | data formatting | bytes 37748736 | tf_op jit(solution)/shard_map/all_gather | solution.py:35
  1001.6 44.8 %multiply_reduce_fusion = (f32[6,192]{1,0:T(8,128)S(1)}, f32[6,192,24576]{2,1,0:T(8,128)}) fusion(bf16[24576,1,6,64]{0,3,2,1:T(8,128)(2,1)} %copy.54, bf16[192,3,6,64]{0,3,2,1:T(8,128)(2,1)S(1)} %add_convert_fusion), kind=kOutput, calls=%fused_computation.6 | convolution fusion | flops 3680500736 | bytes 132321792 | tf_op jit(solution)/shard_map/qhd,khd->hqk/dot_general | solution.py:23
  1046.4 34.9 %fusion.3 = f32[6,192]{1,0:T(8,128)S(1)} fusion(f32[6,192,24576]{2,1,0:T(8,128)} %get-tuple-element.80, f32[6,192]{1,0:T(8,128)S(1)} %get-tuple-element.79), kind=kLoop, calls=%fused_computation.9 | loop fusion | flops 84933504 | bytes 113255424 | tf_op jit(solution)/shard_map/reduce_sum | solution.py:26
  1081.3 8.0 all-gather.29.cloned.1.call-done
  1089.2 48.7 %copy.52 = bf16[24576,1,6,64]{0,3,2,1:T(8,128)(2,1)} copy(bf16[24576,1,6,64]{3,2,1,0:T(8,128)(2,1)} %all-gather.29.cloned.1.call-done) | data formatting | bytes 37748736 | tf_op jit(solution)/shard_map/all_gather | solution.py:36
  1137.9 43.5 %fusion.156 = bf16[192,6,64]{0,2,1:T(8,128)(2,1)S(1)} fusion(f32[6,192,24576]{2,1,0:T(8,128)} %get-tuple-element.80, f32[6,192]{1,0:T(8,128)S(1)} %fusion.3, f32[6,192]{1,0:T(8,128)S(1)} %get-tuple-element.79, bf16[24576,1,6,64]{0,3,2,1:T(8,128)(2,1)} %copy.52), kind=kOutput, calls=%fused_computation.151 | convolution fusion | flops 3737198592 | bytes 132277248 | tf_op jit(solution)/shard_map/hqk,khd->qhd/dot_general | solution.py:27
  1182.2 4.9 fusion.621
  (180 shorter events, 44.8 us)
Async XLA Ops:
  6.5 30.6 %copy-start = (bf16[1536,768]{1,0:T(8,128)(2,1)S(1)}, bf16[1536,768]{1,0:T(8,128)(2,1)}, u32[]{:S(2)}) copy-start(bf16[1536,768]{1,0:T(8,128)(2,1)} %param.25) | copy-start | bytes 7077892
  37.2 1.8 copy-start.10
  45.8 4.9 copy-start.12
  45.8 35.8 %all-to-all-start = ((bf16[64,24,768]{2,1,0:T(8,128)(2,1)}), bf16[64,24,768]{2,1,0:T(8,128)(2,1)S(1)}, u32[]{:S(2)}, u32[]{:S(2)}) async-start(bf16[64,24,768]{2,1,0:T(8,128)(2,1)} %bitcast.331), calls=%async_computation | async-start | bytes 4718592 | tf_op jit(solution)/shard_map/all_to_all | solution.py:69
  50.7 114.6 %all-gather.19.cloned.1.call-start = ((), (), s32[]{:S(2)}) async-start(), calls=%async_computation.3 | async-start | bytes 9510912 | tf_op jit(solution)/shard_map/all_gather | solution.py:35
  86.5 154.4 %all-gather.17.cloned.1.call-start = ((), (), s32[]{:S(2)}) async-start(), calls=%async_computation.2 | async-start | bytes 9510912 | tf_op jit(solution)/shard_map/all_gather | solution.py:36
  87.3 244.0 %all-gather.23.cloned.1.call-start = ((), (), s32[]{:S(2)}) async-start(), calls=%async_computation.5 | async-start | bytes 9510912 | tf_op jit(solution)/shard_map/all_gather | solution.py:35
  254.1 5.0 copy-start.24
  258.4 148.3 %all-gather.21.cloned.1.call-start = ((), (), s32[]{:S(2)}) async-start(), calls=%async_computation.4 | async-start | bytes 9510912 | tf_op jit(solution)/shard_map/all_gather | solution.py:36
  413.9 6.1 copy-start.9
  421.5 7.1 copy-start.32
  421.5 7.1 copy-start.14
  421.5 26.4 %all-to-all-start.1 = ((bf16[64,24,384]{2,1,0:T(8,128)(2,1)}), bf16[64,24,384]{2,1,0:T(8,128)(2,1)S(1)}, u32[]{:S(2)}, u32[]{:S(2)}) async-start(bf16[64,24,384]{2,1,0:T(8,128)(2,1)} %broadcast_select_fusion), calls=%async_computation.1 | async-start | bytes 2359296 | tf_op jit(solution)/shard_map/all_to_all | solution.py:77
  428.5 154.2 %all-gather.27.cloned.1.call-start = ((), (), s32[]{:S(2)}) async-start(), calls=%async_computation.7 | async-start | bytes 50724864 | tf_op jit(solution)/shard_map/all_gather | solution.py:35
  430.2 17.6 %copy-start.11 = (bf16[192,384]{1,0:T(8,128)(2,1)S(1)}, bf16[192,384]{1,0:T(8,128)(2,1)}, u32[]{:S(2)}) copy-start(bf16[192,384]{1,0:T(8,128)(2,1)} %param.24) | copy-start | bytes 442372
  450.3 268.8 %all-gather.25.cloned.1.call-start = ((), (), s32[]{:S(2)}) async-start(), calls=%async_computation.6 | async-start | bytes 50724864 | tf_op jit(solution)/shard_map/all_gather | solution.py:36
  451.3 501.4 %all-gather.31.cloned.1.call-start = ((), (), s32[]{:S(2)}) async-start(), calls=%async_computation.9 | async-start | bytes 50724864 | tf_op jit(solution)/shard_map/all_gather | solution.py:35
  767.7 43.4 %copy-start.3 = (f32[192,384]{1,0:T(8,128)S(1)}, f32[192,384]{1,0:T(8,128)}, u32[]{:S(2)}) copy-start(f32[192,384]{1,0:T(8,128)} %copy-done.2) | copy-start | bytes 884740
  767.7 43.4 %copy-start.7 = (bf16[2,6,64,384]{3,2,1,0:T(8,128)(2,1)S(1)}, bf16[2,6,64,384]{3,2,1,0:T(8,128)(2,1)}, u32[]{:S(2)}) copy-start(bf16[2,6,64,384]{3,2,1,0:T(8,128)(2,1)} %param.37) | copy-start | bytes 1769476
  767.8 43.4 %copy-start.17 = (f32[384]{0:T(512)S(1)}, f32[384]{0:T(512)}, u32[]{:S(2)}) copy-start(f32[384]{0:T(512)} %get-tuple-element.31) | copy-start | bytes 4612
  811.8 5.3 copy-start.4
  811.8 5.3 copy-start.22
  811.8 5.3 copy-start.23
  818.1 2.1 copy-start.15
  818.1 2.7 copy-start.25
  819.1 270.2 %all-gather.29.cloned.1.call-start = ((), (), s32[]{:S(2)}) async-start(), calls=%async_computation.8 | async-start | bytes 50724864 | tf_op jit(solution)/shard_map/all_gather | solution.py:36
  1137.9 43.6 %copy-start.6 = (f32[192,384]{1,0:T(8,128)S(1)}, f32[192,384]{1,0:T(8,128)}, u32[]{:S(2)}) copy-start(f32[192,384]{1,0:T(8,128)} %copy-done.5) | copy-start | bytes 884740
  1137.9 43.6 %copy-start.8 = (bf16[2,6,64,384]{3,2,1,0:T(8,128)(2,1)S(1)}, bf16[2,6,64,384]{3,2,1,0:T(8,128)(2,1)}, u32[]{:S(2)}) copy-start(bf16[2,6,64,384]{3,2,1,0:T(8,128)(2,1)} %param.37) | copy-start | bytes 1769476
  1137.9 43.6 %copy-start.16 = (f32[384]{0:T(512)S(1)}, f32[384]{0:T(512)}, u32[]{:S(2)}) copy-start(f32[384]{0:T(512)} %get-tuple-element.23) | copy-start | bytes 4612
  1182.2 5.2 copy-start.18
  1182.2 5.2 copy-start.19
  1187.4 3.0 copy-start.1
  (11 other events, 7.9 us)
Sparse Core Ops, SparseCore 0:
  86.6 78.6 all-gather.18
  168.2 72.6 all-gather.16
  258.5 72.6 all-gather.22
  333.9 72.6 all-gather.20
  450.4 132.2 all-gather.26
  585.6 133.3 all-gather.24
  819.2 133.4 all-gather.30
  955.8 133.3 all-gather.28
where the time goes:
time: 1210 us; the launch traced here: 1200 us
  waiting for transfers between devices  608 us (50%)
  matrix products  243 us (20%)
  local copies, waits for them, and re-layouts  218 us (18%)
  other arithmetic  78.2 us (6%)
  blocking collectives  20.9 us (2%)
  between operations  16.4 us (1%)
  starting transfers between devices  12.8 us (1%)
    all_gather x4, waiting for transfers between devices, run_block(): key_rows = gather_rows(qkv_rows[:, 1])  411 us
    all_gather x4, waiting for transfers between devices, run_block(): value_rows = gather_rows(qkv_rows[:, 2])  151 us
    all_gather x2, local copies, waits for them, and re-layouts, run_block(): key_rows = gather_rows(qkv_rows[:, 1])  97.5 us
    all_gather x2, local copies, waits for them, and re-layouts, run_block(): value_rows = gather_rows(qkv_rows[:, 2])  97.4 us
    dot_general x2, matrix products, attend(): jnp.einsum('qhd,khd->hqk', query_rows, key_rows, preferred_element_type=j...  89.6 us
    dot_general x2, matrix products, attend(): jnp.einsum('hqk,khd->qhd', attn_probs, value_rows, preferred_element_type...  86.9 us
    reduce_sum x2, other arithmetic, attend(): attn_probs = jax.nn.softmax(scores, axis=-1).astype(jnp.bfloat16)  69.7 us
    all_to_all x1, waiting for transfers between devices, local_step(): received = lax.all_to_all(send_rows, 'region', 0, 0, tiled=True)  30.3 us
  transfers between devices with their start and end apart: 10, of which 10 were waited for; matrix products, arithmetic and copies ran while one was open for 24% of the time, Pallas kernels for 0%

commit v1 on v0

v1 whole, which is shorter than its diff:
```python
import functools
import jax
import jax.numpy as jnp
from jax import lax
from jax.experimental import pallas as pl
from jax.experimental.pallas import tpu as pltpu
from jax.sharding import PartitionSpec as P

LN_EPS = 1e-6
TOKEN_AXES = ("batch", "time", "region")
SIDE = 4
REGIONS = SIDE ** 3
PLANE = SIDE * SIDE * 2
ROW = SIDE * 2
HEAD = 64
MESH = pl.DeviceIdType.MESH
RING = (1, 3, 2)
VMEM_LIMIT = 60 * 1024 * 1024


def position():
    t, r = lax.axis_index("time"), lax.axis_index("region")
    return t, r // 16, lax.rem(r // 4, 4), lax.rem(r, 4)


def device(t, z, y, x):
    return {"time": t, "region": z * 16 + y * 4 + x}


def turn(a, d):
    return lax.rem(a + d, SIDE)


def gather_kernel(a_ref, b_ref, q_ref, kv_ref, qall_ref, a_send, a_recv, b_send, b_recv, q_send, q_recv):
    t, z, y, x = position()
    other = 1 - t
    barrier = pltpu.get_barrier_semaphore()
    peers = [(other, z, y, x)]
    for d in RING:
        for c in range(2):
            peers += [(c, turn(z, d), y, x), (c, z, turn(y, d), x), (c, z, y, turn(x, d))]
    for peer in peers:
        pl.semaphore_signal(barrier, inc=1, device_id=device(*peer), device_id_type=MESH)
    pl.semaphore_wait(barrier, len(peers))

    def slot(z_, y_, t_):
        return (z_ * SIDE + y_) * 2 + t_

    mine = slot(z, y, t)
    row_mine = x * 2 + t
    sends = []
    counts = {"a": 0, "b": 0, "q": 0}
    send_sems = {"a": a_send, "b": b_send, "q": q_send}
    recv_sems = {"a": a_recv, "b": b_recv, "q": q_recv}
    dests = {"a": kv_ref.at[0], "b": kv_ref.at[1], "q": qall_ref}
    sources = {"a": a_ref, "b": b_ref, "q": q_ref}

    def send(kind, src, to_slot, peer):
        copy = pltpu.make_async_remote_copy(
            src_ref=src,
            dst_ref=dests[kind].at[to_slot],
            send_sem=send_sems[kind].at[counts[kind]],
            recv_sem=recv_sems[kind].at[to_slot],
            device_id=device(*peer),
            device_id_type=MESH,
        )
        counts[kind] += 1
        copy.start()
        sends.append(copy)

    def arrived(kind, at):
        pltpu.make_async_remote_copy(
            src_ref=dests[kind].at[at],
            dst_ref=dests[kind].at[at],
            send_sem=send_sems[kind].at[0],
            recv_sem=recv_sems[kind].at[at],
            device_id=device(t, z, y, x),
            device_id_type=MESH,
        ).wait_recv()

    send("q", q_ref.at[other], row_mine, (other, z, y, x))
    send("a", a_ref.at[other], mine, (other, z, y, x))
    send("b", b_ref.at[other], mine, (other, z, y, x))
    for d in RING:
        for c in range(2):
            send("q", q_ref.at[c], row_mine, (c, z, y, turn(x, d)))
            send("a", a_ref.at[c], mine, (c, z, turn(y, d), x))
            send("b", b_ref.at[c], mine, (c, turn(z, d), y, x))
    for d in RING:
        send("a", a_ref.at[t], mine, (t, turn(z, d), y, x))
        send("b", b_ref.at[t], mine, (t, z, turn(y, d), x))
    kv_ref[0, mine] = a_ref[t]
    kv_ref[1, mine] = b_ref[t]
    qall_ref[row_mine] = q_ref[t]

    arrivals = [(0, other)] + [(4 - d, c) for d in RING for c in range(2)]
    for d0, c in arrivals:
        at = slot(z, turn(y, d0), c)
        arrived("a", at)
        for d in RING:
            send("a", dests["a"].at[at], at, (t, turn(z, d), y, x))
        at = slot(turn(z, d0), y, c)
        arrived("b", at)
        for d in RING:
            send("b", dests["b"].at[at], at, (t, z, turn(y, d), x))
    for dz in RING:
        for dy in range(SIDE):
            for c in range(2):
                arrived("a", slot(turn(z, dz), turn(y, dy), c))
                arrived("b", slot(turn(z, dy), turn(y, dz), c))
    for d0, c in arrivals:
        arrived("q", turn(x, d0) * 2 + c)
    for copy in sends:
        copy.wait_send()


def gather(a, b, q, collective_id):
    halves, rows, lanes = a.shape
    n = 31
    vmem = pl.BlockSpec(memory_space=pltpu.VMEM)
    return pl.pallas_call(
        gather_kernel,
        out_shape=(
            jax.ShapeDtypeStruct((2, PLANE, rows, lanes), a.dtype),
            jax.ShapeDtypeStruct((ROW,) + q.shape[1:], q.dtype),
        ),
        in_specs=[vmem] * 3,
        out_specs=(vmem, vmem),
        scratch_shapes=[
            pltpu.SemaphoreType.DMA((n,)),
            pltpu.SemaphoreType.DMA((PLANE,)),
            pltpu.SemaphoreType.DMA((n,)),
            pltpu.SemaphoreType.DMA((PLANE,)),
            pltpu.SemaphoreType.DMA((ROW,)),
            pltpu.SemaphoreType.DMA((ROW,)),
        ],
        compiler_params=pltpu.CompilerParams(collective_id=collective_id, has_side_effects=True, vmem_limit_bytes=VMEM_LIMIT),
        name="gather_kv",
    )(a, b, q)


def flash_kernel(heads, key_block, steps, q_ref, k_ref, vt_ref, out_ref, acc_ref, stat_ref):
    width = heads * HEAD
    acc_ref[...] = jnp.zeros_like(acc_ref)
    lanes = q_ref.shape[-1]
    for h in range(heads):
        stat_ref[h] = jnp.full((8, lanes), -jnp.inf, jnp.float32)
        stat_ref[heads + h] = jnp.zeros((8, lanes), jnp.float32)

    def step(i, _):
        at = pl.multiple_of(i * key_block, key_block)
        for h in range(heads):
            k_rows = k_ref[pl.ds(at, key_block), (h // 2) * 128:(h // 2 + 1) * 128]
            scores = jnp.dot(k_rows, q_ref[h], preferred_element_type=jnp.float32)
            old = stat_ref[h, 0:1]
            new = jnp.maximum(old, jnp.max(scores, axis=0, keepdims=True))
            weights = jnp.exp(scores - new)
            fade = jnp.exp(old - new)
            stat_ref[h, 0:1] = new
            stat_ref[heads + h, 0:1] = stat_ref[heads + h, 0:1] * fade + jnp.sum(weights, axis=0, keepdims=True)
            part = jnp.dot(vt_ref[h * HEAD:(h + 1) * HEAD, pl.ds(at, key_block)], weights.astype(jnp.bfloat16), preferred_element_type=jnp.float32)
            acc_ref[h * HEAD:(h + 1) * HEAD] = acc_ref[h * HEAD:(h + 1) * HEAD] * fade + part
        return 0

    lax.fori_loop(0, steps, step, 0)
    for h in range(heads):
        acc_ref[width + h:width + h + 1] = stat_ref[h, 0:1]
        acc_ref[width + heads + h:width + heads + h + 1] = stat_ref[heads + h, 0:1]
    out_ref[...] = acc_ref[...].T


def flash(q, k, vt, key_block):
    heads, _, queries = q.shape
    keys, lanes = k.shape
    out_lanes = -(-(heads * HEAD + 2 * heads) // 128) * 128
    block = 256
    return pl.pallas_call(
        functools.partial(flash_kernel, heads, key_block, keys // key_block),
        grid=(queries // block,),
        out_shape=jax.ShapeDtypeStruct((queries, out_lanes), jnp.float32),
        in_specs=[
            pl.BlockSpec((heads, 128, block), lambda i: (0, 0, i)),
            pl.BlockSpec((keys, lanes), lambda i: (0, 0)),
            pl.BlockSpec((heads * HEAD, keys), lambda i: (0, 0)),
        ],
        out_specs=pl.BlockSpec((block, out_lanes), lambda i: (i, 0)),
        scratch_shapes=[pltpu.VMEM((out_lanes, block), jnp.float32), pltpu.VMEM((2 * heads, 8, block), jnp.float32)],
        compiler_params=pltpu.CompilerParams(vmem_limit_bytes=VMEM_LIMIT),
        name="flash",
    )(q, k, vt)


def combine_kernel(heads, part_ref, out_ref, got_ref, send_sem, recv_sem):
    t, z, y, x = position()
    barrier = pltpu.get_barrier_semaphore()
    peers = [(1 - t, z, y, x)] + [(c, z, y, turn(x, d)) for d in RING for c in range(2)]
    for peer in peers:
        pl.semaphore_signal(barrier, inc=1, device_id=device(*peer), device_id_type=MESH)
    pl.semaphore_wait(barrier, len(peers))
    mine = x * 2 + t
    sends = []
    for i, peer in enumerate(peers):
        copy = pltpu.make_async_remote_copy(
            src_ref=part_ref.at[peer[3] * 2 + peer[0]],
            dst_ref=got_ref.at[mine],
            send_sem=send_sem.at[i],
            recv_sem=recv_sem.at[mine],
            device_id=device(*peer),
            device_id_type=MESH,
        )
        copy.start()
        sends.append(copy)
    got_ref[mine] = part_ref[mine]
    for peer in peers:
        at = peer[3] * 2 + peer[0]
        pltpu.make_async_remote_copy(
            src_ref=got_ref.at[at],
            dst_ref=got_ref.at[at],
            send_sem=send_sem.at[0],
            recv_sem=recv_sem.at[at],
            device_id=device(t, z, y, x),
            device_id_type=MESH,
        ).wait_recv()
    width = heads * HEAD
    tokens = part_ref.shape[1]
    out_width = out_ref.shape[-1]
    head_of = lax.broadcasted_iota(jnp.int32, (tokens, out_width), 1) // HEAD

    def spread(columns):
        full = jnp.broadcast_to(columns[:, 0:1], (tokens, out_width))
        for h in range(1, heads):
            full = jnp.where(head_of == h, columns[:, h:h + 1], full)
        return full

    for c in range(2):
        blocks = [got_ref[2 * i + c] for i in range(SIDE)]
        tops = [b[:, width:width + heads] for b in blocks]
        top = functools.reduce(jnp.maximum, tops)
        fades = [jnp.exp(m - top) for m in tops]
        total = sum(f * b[:, width + heads:width + 2 * heads] for f, b in zip(fades, blocks))
        merged = sum(spread(f / total) * b[:, :out_width] for f, b in zip(fades, blocks))
        out_ref[c] = jnp.where(head_of < heads, merged, 0.0).astype(jnp.bfloat16)
    for copy in sends:
        copy.wait_send()


def combine(parts, heads, collective_id):
    _, tokens, lanes = parts.shape
    out_width = -(-heads * HEAD // 128) * 128
    vmem = pl.BlockSpec(memory_space=pltpu.VMEM)
    out = pl.pallas_call(
        functools.partial(combine_kernel, heads),
        out_shape=jax.ShapeDtypeStruct((2, tokens, out_width), jnp.bfloat16),
        in_specs=[vmem],
        out_specs=vmem,
        scratch_shapes=[
            pltpu.VMEM(parts.shape, jnp.float32),
            pltpu.SemaphoreType.DMA((ROW,)),
            pltpu.SemaphoreType.DMA((ROW,)),
        ],
        compiler_params=pltpu.CompilerParams(collective_id=collective_id, has_side_effects=True, vmem_limit_bytes=VMEM_LIMIT),
        name="combine",
    )(parts)
    return out[:, :, :heads * HEAD]


def exchange_kernel(spread, src_ref, dst_ref, send_sem, recv_sem):
    t, me = lax.axis_index("time"), lax.axis_index("region")
    barrier = pltpu.get_barrier_semaphore()

    def signal(d, _):
        pl.semaphore_signal(barrier, inc=1, device_id={"time": t, "region": lax.rem(me + d, REGIONS)}, device_id_type=MESH)
        return 0

    lax.fori_loop(1, REGIONS, signal, 0)
    pl.semaphore_wait(barrier, REGIONS - 1)

    def copy_to(peer, slot):
        return pltpu.make_async_remote_copy(
            src_ref=src_ref if spread else src_ref.at[peer],
            dst_ref=dst_ref.at[slot],
            send_sem=send_sem.at[peer],
            recv_sem=recv_sem.at[slot],
            device_id={"time": t, "region": peer},
            device_id_type=MESH,
        )

    def start(d, _):
        copy_to(lax.rem(me + d, REGIONS), me).start()
        return 0

    lax.fori_loop(1, REGIONS, start, 0)
    dst_ref[me] = src_ref[...] if spread else src_ref[me]

    def finish(d, _):
        peer = lax.rem(me + d, REGIONS)
        copy_to(peer, peer).wait_recv()
        return 0

    lax.fori_loop(1, REGIONS, finish, 0)

    def drain(d, _):
        copy_to(lax.rem(me + d, REGIONS), me).wait_send()
        return 0

    lax.fori_loop(1, REGIONS, drain, 0)


def exchange(rows, spread, collective_id):
    block = rows.shape if spread else rows.shape[1:]
    vmem = pl.BlockSpec(memory_space=pltpu.VMEM)
    return pl.pallas_call(
        functools.partial(exchange_kernel, spread),
        out_shape=jax.ShapeDtypeStruct((REGIONS,) + block, rows.dtype),
        in_specs=[vmem],
        out_specs=vmem,
        scratch_shapes=[pltpu.SemaphoreType.DMA((REGIONS,)), pltpu.SemaphoreType.DMA((REGIONS,))],
        compiler_params=pltpu.CompilerParams(collective_id=collective_id, has_side_effects=True),
        name="exchange",
    )(rows)


def layer_norm(hidden, ln_gain, ln_shift):
    hid_f32 = hidden.astype(jnp.float32)
    mean_val = jnp.mean(hid_f32, axis=-1, keepdims=True)
    centered = hid_f32 - mean_val
    variance = jnp.mean(centered * centered, axis=-1, keepdims=True)
    return centered * lax.rsqrt(variance + LN_EPS) * ln_gain + ln_shift


def run_block(hidden, vec_rows, w_qkv, w_o, w_one, w_two, key_block, collective_id):
    tokens, width = hidden.shape
    heads = w_qkv.shape[2] // 2
    half = heads * HEAD
    normed = layer_norm(hidden, vec_rows[0], vec_rows[1]).astype(jnp.bfloat16)
    w_rows = w_qkv.transpose(1, 2, 3, 0).reshape(3 * width, width)
    projected = lax.dot_general(normed, w_rows, (((1,), (1,)), ((), ())), preferred_element_type=jnp.float32)
    bias = jnp.concatenate([vec_rows[4], jnp.zeros_like(vec_rows[4]), vec_rows[5]])
    projected = (projected + bias).astype(jnp.bfloat16)

    def halves(part):
        return jnp.stack([projected[:, part * width + c * half:part * width + (c + 1) * half] for c in range(2)])

    q, k, v = halves(0) * jnp.bfloat16(HEAD ** -0.5), halves(1), halves(2)
    if half % 128 == 0:
        a, b = k, v
    else:
        both = jnp.concatenate([k, v], axis=-1)
        a, b = both[:, :tokens // 2], both[:, tokens // 2:]
    kv_all, q_all = gather(a, b, q, collective_id)
    if half % 128 == 0:
        keys = kv_all[0].reshape(-1, half)
        values_t = kv_all[1].reshape(-1, half).T
    else:
        keys = kv_all.reshape(-1, 2 * half)
        values_t = keys[:, half:].T
    count = ROW * tokens
    queries = q_all.reshape(count, heads, HEAD).transpose(1, 2, 0)
    padded = -(-count // 256) * 256
    rows = jnp.arange(heads) % 2
    zeros = jnp.zeros_like(queries)
    even = jnp.concatenate([queries, zeros], axis=1)
    odd = jnp.concatenate([zeros, queries], axis=1)
    queries = jnp.where((rows == 0)[:, None, None], even, odd)
    queries = jnp.pad(queries, ((0, 0), (0, 0), (0, padded - count)))
    parts = flash(queries, keys, values_t, key_block)[:count].reshape(ROW, tokens, -1)
    attended = combine(parts, heads, collective_id + 1)
    w_o = w_o.reshape(2, half, width)
    mixed = sum(jnp.dot(attended[c], w_o[c], preferred_element_type=jnp.float32) for c in range(2))
    residual = (hidden.astype(jnp.float32) + mixed + vec_rows[6]).astype(jnp.bfloat16)
    normed_mlp = layer_norm(residual, vec_rows[2], vec_rows[3]).astype(jnp.bfloat16)
    mlp_hidden = jax.nn.gelu(jnp.dot(normed_mlp, w_one, preferred_element_type=jnp.float32) + vec_rows[8:12].reshape(-1), approximate=False).astype(jnp.bfloat16)
    return (residual.astype(jnp.float32) + jnp.dot(mlp_hidden, w_two, preferred_element_type=jnp.float32) + vec_rows[7]).astype(jnp.bfloat16)


def one_hot_rows(selector, rows):
    return jnp.dot(selector.astype(jnp.bfloat16), rows, preferred_element_type=jnp.float32).astype(jnp.bfloat16)


def solution(mesh):
    def local_step(patches, enc_pos, vis_mask, dec_pos, w_embed, b_embed, enc_vec, enc_wqkv, enc_wo, enc_w1, enc_w2, enc_final, w_dec_in, mask_token, dec_vec, dec_wqkv, dec_wo, dec_w1, dec_w2, dec_final, w_out):
        tokens = patches.shape[0]
        per_dev = tokens // 8
        me = lax.axis_index("region")
        own_count = jnp.sum(vis_mask)
        counts = exchange(jnp.full((8, 128), own_count, jnp.int32), True, 1)[:, 0, 0]
        embedded = (jnp.dot(patches, w_embed, preferred_element_type=jnp.float32) + b_embed + enc_pos.astype(jnp.float32)).astype(jnp.bfloat16)

        region_ids = jnp.arange(REGIONS, dtype=jnp.int32)
        starts = jnp.sum(jnp.where(region_ids[None, :] < region_ids[:, None], counts[None, :], 0), axis=1)
        start = jnp.sum(jnp.where(region_ids < me, counts, 0))
        token_ids = jnp.arange(tokens, dtype=jnp.int32)
        local_rank = jnp.sum(jnp.where(token_ids[None, :] < token_ids[:, None], vis_mask[None, :], 0), axis=1)
        send_row = jnp.where(vis_mask == 1, lax.rem(start + local_rank, REGIONS) * 2 + local_rank // REGIONS, -1)
        row_ids = jnp.arange(2 * REGIONS, dtype=jnp.int32)
        deal = row_ids[:, None] == send_row[None, :]
        source_starts, source_counts = jnp.repeat(starts, 2), jnp.repeat(counts, 2)
        rank = lax.rem(me - lax.rem(source_starts, REGIONS) + REGIONS, REGIONS) + REGIONS * lax.rem(row_ids, 2)
        place = jnp.where(rank < source_counts, (source_starts + rank) // REGIONS, -1)
        pack = jnp.arange(per_dev, dtype=jnp.int32)[:, None] == place[None, :]

        sent = one_hot_rows(deal, embedded).reshape(REGIONS, 2, -1)
        hidden = one_hot_rows(pack, exchange(sent, False, 2).reshape(2 * REGIONS, -1))
        for layer in range(enc_vec.shape[0]):
            hidden = run_block(hidden, enc_vec[layer], enc_wqkv[layer], enc_wo[layer], enc_w1[layer], enc_w2[layer], 768, 4 + 2 * layer)
        latent = jnp.dot(layer_norm(hidden, enc_final[0], enc_final[1]).astype(jnp.bfloat16), w_dec_in, preferred_element_type=jnp.float32).astype(jnp.bfloat16)
        back = one_hot_rows(pack.T, latent).reshape(REGIONS, 2, -1)
        returned = exchange(back, False, 3).reshape(2 * REGIONS, -1)
        placed = jnp.dot(deal.T.astype(jnp.bfloat16), returned, preferred_element_type=jnp.float32)
        hidden = (jnp.where(vis_mask[:, None] == 1, placed, mask_token.astype(jnp.float32)) + dec_pos.astype(jnp.float32)).astype(jnp.bfloat16)
        for layer in range(dec_vec.shape[0]):
            hidden = run_block(hidden, dec_vec[layer], dec_wqkv[layer], dec_wo[layer], dec_w1[layer], dec_w2[layer], 512, 8 + 2 * layer)
        return jnp.dot(layer_norm(hidden, dec_final[0], dec_final[1]).astype(jnp.bfloat16), w_out, preferred_element_type=jnp.float32)

    token_rows = P(TOKEN_AXES, None)
    token_flags = P(TOKEN_AXES)
    replicated = P()
    in_specs = (token_rows, token_rows, token_flags, token_rows) + (replicated,) * 17
    return jax.shard_map(local_step, mesh=mesh, in_specs=in_specs, out_specs=token_rows, check_vma=False)
```

time: 1210 us -> 556 us (0.46)
  waiting for transfers between devices: 608 us -> 0 us
  Pallas kernels: 0 us -> 438 us
  matrix products: 243 us -> 38 us
  local copies, waits for them, and re-layouts: 218 us -> 56.6 us
  other arithmetic: 78.2 us -> 18.4 us
  blocking collectives: 20.9 us -> 0 us
  between operations: 16.4 us -> 1.06 us
  starting transfers between devices: 12.8 us -> 0 us
    all_gather x8 -> x0, waiting for transfers between devices: 562 us -> none  [the longest x4 411 us: run_block(): key_rows = gather_rows(qkv_rows[:, 1])]
    pallas_call x0 -> x15, Pallas kernels: none -> 438 us  [the longest x4 203 us: flash(): pl.pallas_call(functools.partial(flash_kernel, heads, key_block, keys //...]
    all_gather x4 -> x0, local copies, waits for them, and re-layouts: 195 us -> none  [the longest x2 97.5 us: run_block(): key_rows = gather_rows(qkv_rows[:, 1])]
    dot_general x14 -> x16, matrix products: 201 us -> 12.2 us  [the longest x8 5.19 us: run_block(): jnp.dot(attended[c], w_o[c], preferred_element_type=jnp.float32)]
    reduce_sum x4 -> x3, other arithmetic: 70.2 us -> 1.53 us  [the longest x1 0.78 us: local_step(): jnp.sum(jnp.where(token_ids[None, :] < token_ids[:, None], vis_mask[None,...]
    all_to_all x2 -> x0, waiting for transfers between devices: 45.3 us -> none  [the longest x1 30.3 us: local_step(): received = lax.all_to_all(send_rows, 'region', 0, 0, tiled=True)]
    unnamed x1 -> x0, blocking collectives: 20.9 us -> none
    sub x2 -> x0, matrix products: 16.4 us -> none  [attend(): attn_probs = jax.nn.softmax(scores, axis=-1).astype(jnp.bfloat16)]
  transfers between devices with their start and end apart: 10 -> 0, of which waited for: 10 -> 0; matrix products, arithmetic and copies ran while one was open for 24% -> 0% of each run, Pallas kernels for 0% -> 0%
where the time goes in v1:
time: 556 us; the launch traced here: 552 us
  Pallas kernels  438 us (79%)
  local copies, waits for them, and re-layouts  56.6 us (10%)
  matrix products  38 us (7%)
  other arithmetic  18.4 us (3%)
    pallas_call x4, Pallas kernels, flash(): pl.pallas_call(functools.partial(flash_kernel, heads, key_block, keys //...  203 us
    pallas_call x4, Pallas kernels, gather(): pl.pallas_call(gather_kernel, out_shape=(jax.ShapeDtypeStruct((2, PLANE,...  118 us
    pallas_call x4, Pallas kernels, combine(): pl.pallas_call(functools.partial(combine_kernel, heads), out_shape=jax.Sh...  73 us
    pallas_call x3, Pallas kernels, exchange(): pl.pallas_call(functools.partial(exchange_kernel, spread), out_shape=jax....  44.4 us
    dot_general x4, matrix products, run_block(): jnp.dot(mlp_hidden, w_two, preferred_element_type=jnp.float32)  22.8 us

profile of v1, /device:TPU:1, one launch (start us, length us, event | category | flops | bytes accessed | tf_op | source)
XLA Modules:
  0.0 552.2 jit_solution(1064345279363566378)
XLA Ops:
  5.0 17.5 %exchange.3 = s32[64,8,128]{2,1,0:T(8,128)} custom-call(s32[8,128]{1,0:T(8,128)} %broadcast_in_dim.77.src_ref), custom_call_target="tpu_custom_call" | custom-call | tf_op jit(solution)/shard_map/exchange/pallas_call | solution.py:312
  22.5 2.2 slice_reduce_fusion
  28.7 2.0 convolution_convert_fusion
  31.5 13.9 %exchange.4 = bf16[64,2,768]{2,1,0:T(2,128)(2,1)} custom-call(bf16[64,2,768]{2,1,0:T(2,128)(2,1)} %reshape.359.src_ref), custom_call_target="tpu_custom_call" | custom-call | tf_op jit(solution)/shard_map/exchange/pallas_call | solution.py:312
  46.9 3.6 fusion.505
  52.8 20.6 %gather_kv.4 = (bf16[2,32,24,384]{3,2,1,0:T(8,128)(2,1)}, bf16[8,24,384]{2,1,0:T(8,128)(2,1)}) custom-call(bf16[2,24,384]{2,1,0:T(8,128)(2,1)} %get-tuple-element.131.a_ref, bf16[2,24,384]{2,1,0:T(8,128)(2,1)} %get-tuple-element.132.b_ref, bf16[2,24,384]{2,1,0:T(8,128)(2,1)} %maximum_multiply_fusion.2.q_ref), custom_call_target="tpu_custom_call" | custom-call | tf_op jit(solution)/shard_map/gather_kv/pallas_call | solution.py:121
  73.5 2.4 fusion.509
  75.9 2.1 copy.41
  83.8 5.4 flash.4
  91.0 10.9 %combine.4 = bf16[2,24,384]{2,1,0:T(8,128)(2,1)} custom-call(f32[8,24,512]{2,1,0:T(8,128)} %bitcast.266), custom_call_target="tpu_custom_call" | custom-call | tf_op jit(solution)/shard_map/combine/pallas_call | solution.py:251
  101.9 2.9 fusion.506
  108.1 7.0 %fusion.516 = (f32[24]{0:T(128)}, f32[24,768]{1,0:T(8,128)}) fusion(f32[768]{0:T(1024)} %get-tuple-element.28, f32[24,768]{1,0:T(8,128)} %copy-done.14, bf16[2,3072,768]{2,1,0:T(8,128)(2,1)} %param.31, bf16[2,768,3072]{2,1,0:T(8,128)(2,1)} %param.30, f32[3072]{0:T(1024)} %bitcast.275, f32[768]{0:T(1024)} %get-tuple-element.29, f32[768]{0:T(1024)} %get-tuple-element.30, ...), kind=kOutput, calls=%fused_computation.642 | convolution fusion | flops 231542752 | bytes 9684064 | tf_op jit(solution)/shard_map/dot_general | solution.py:373
  116.9 2.0 fusion.19
  120.8 15.9 %gather_kv.5 = (bf16[2,32,24,384]{3,2,1,0:T(8,128)(2,1)}, bf16[8,24,384]{2,1,0:T(8,128)(2,1)}) custom-call(bf16[2,24,384]{2,1,0:T(8,128)(2,1)} %pad_maximum_fusion.2.a_ref, bf16[2,24,384]{2,1,0:T(8,128)(2,1)} %pad_maximum_fusion.3.b_ref, bf16[2,24,384]{2,1,0:T(8,128)(2,1)} %maximum_multiply_fusion.3.q_ref), custom_call_target="tpu_custom_call" | custom-call | tf_op jit(solution)/shard_map/gather_kv/pallas_call | solution.py:121
  136.7 2.2 fusion.508
  141.4 5.7 %flash.5 = f32[256,512]{1,0:T(8,128)} custom-call(bf16[6,128,256]{2,1,0:T(8,128)(2,1)} %pad.16.q_ref, bf16[768,384]{1,0:T(8,128)(2,1)} %bitcast.262, bf16[384,768]{1,0:T(8,128)(2,1)} %bitcast.258), custom_call_target="tpu_custom_call" | custom-call | tf_op jit(solution)/shard_map/flash/pallas_call | solution.py:177
  148.9 10.9 %combine.5 = bf16[2,24,384]{2,1,0:T(8,128)(2,1)} custom-call(f32[8,24,512]{2,1,0:T(8,128)} %bitcast.267), custom_call_target="tpu_custom_call" | custom-call | tf_op jit(solution)/shard_map/combine/pallas_call | solution.py:251
  162.1 5.8 %fusion.520 = (f32[24]{0:T(128)S(1)}, f32[24,768]{1,0:T(8,128)S(1)}) fusion(f32[768]{0:T(1024)S(1)} %copy-done.31, f32[24,768]{1,0:T(8,128)S(1)} %get-tuple-element.118, bf16[2,3072,768]{2,1,0:T(8,128)(2,1)} %param.31, bf16[2,768,3072]{2,1,0:T(8,128)(2,1)} %param.30, f32[3072]{0:T(1024)S(1)} %bitcast.274, f32[768]{0:T(1024)S(1)} %copy-done.30, ...), kind=kOutput, calls=%fused_computation.644 | convolution fusion | flops 231542752 | bytes 9684064 | tf_op jit(solution)/shard_map/dot_general | solution.py:373
  169.4 13.0 %exchange.5 = bf16[64,2,384]{2,1,0:T(2,128)(2,1)} custom-call(bf16[64,2,384]{2,1,0:T(2,128)(2,1)} %reshape.367.src_ref), custom_call_target="tpu_custom_call" | custom-call | tf_op jit(solution)/shard_map/exchange/pallas_call | solution.py:312
  187.5 41.4 %gather_kv.6 = (bf16[2,32,96,384]{3,2,1,0:T(8,128)(2,1)}, bf16[8,192,192]{2,1,0:T(8,128)(2,1)}) custom-call(bf16[2,96,384]{2,1,0:T(8,128)(2,1)} %get-tuple-element.92.a_ref, bf16[2,96,384]{2,1,0:T(8,128)(2,1)} %get-tuple-element.91.b_ref, bf16[2,192,192]{2,1,0:T(8,128)(2,1)} %maximum_multiply_fusion.q_ref), custom_call_target="tpu_custom_call" | custom-call | tf_op jit(solution)/shard_map/gather_kv/pallas_call | solution.py:121
  228.9 3.6 slice.544
  232.5 2.7 copy.48
  239.1 95.9 %flash.6 = f32[1536,256]{1,0:T(8,128)} custom-call(bf16[3,128,1536]{2,1,0:T(8,128)(2,1)} %pad_select_fusion.1.q_ref, bf16[6144,384]{1,0:T(8,128)(2,1)} %bitcast.245, bf16[192,6144]{1,0:T(8,128)(2,1)} %bitcast.248), custom_call_target="tpu_custom_call" | custom-call | tf_op jit(solution)/shard_map/flash/pallas_call | solution.py:177
  335.0 25.6 %combine.6 = bf16[2,192,256]{2,1,0:T(8,128)(2,1)} custom-call(f32[8,192,256]{2,1,0:T(8,128)} %bitcast.250), custom_call_target="tpu_custom_call" | custom-call | tf_op jit(solution)/shard_map/combine/pallas_call | solution.py:251
  362.3 5.0 fusion.525
  369.8 40.1 %gather_kv.7 = (bf16[2,32,96,384]{3,2,1,0:T(8,128)(2,1)}, bf16[8,192,192]{2,1,0:T(8,128)(2,1)}) custom-call(bf16[2,96,384]{2,1,0:T(8,128)(2,1)} %get-tuple-element.90.a_ref, bf16[2,96,384]{2,1,0:T(8,128)(2,1)} %get-tuple-element.89.b_ref, bf16[2,192,192]{2,1,0:T(8,128)(2,1)} %maximum_multiply_fusion.1.q_ref), custom_call_target="tpu_custom_call" | custom-call | tf_op jit(solution)/shard_map/gather_kv/pallas_call | solution.py:121
  409.9 3.6 slice.553
  413.5 2.7 copy.49
  420.0 95.7 %flash.7 = f32[1536,256]{1,0:T(8,128)} custom-call(bf16[3,128,1536]{2,1,0:T(8,128)(2,1)} %pad_select_fusion.q_ref, bf16[6144,384]{1,0:T(8,128)(2,1)} %bitcast.247, bf16[192,6144]{1,0:T(8,128)(2,1)} %bitcast.249), custom_call_target="tpu_custom_call" | custom-call | tf_op jit(solution)/shard_map/flash/pallas_call | solution.py:177
  515.7 25.6 %combine.7 = bf16[2,192,256]{2,1,0:T(8,128)(2,1)} custom-call(f32[8,192,256]{2,1,0:T(8,128)} %bitcast.251), custom_call_target="tpu_custom_call" | custom-call | tf_op jit(solution)/shard_map/combine/pallas_call | solution.py:251
  543.9 4.9 fusion.529
  549.1 3.0 fusion.222
  (184 shorter events, 55.4 us)
Async XLA Ops:
  0.0 28.7 %copy-start = (bf16[1536,768]{1,0:T(8,128)(2,1)S(1)}, bf16[1536,768]{1,0:T(8,128)(2,1)}, u32[]{:S(2)}) copy-start(bf16[1536,768]{1,0:T(8,128)(2,1)} %param.25) | copy-start | bytes 7077892
  25.4 21.0 %copy-start.25 = (s32[128]{0:T(128)}, s32[128]{0:T(128)S(1)}, u32[]{:S(2)}) copy-start(s32[128]{0:T(128)S(1)} %compare_select_fusion.6) | copy-start | bytes 1540
  28.7 2.0 copy-start.27
  46.6 3.8 copy-start.6
  46.8 3.6 copy-start.18
  46.8 3.6 copy-start.21
  46.9 3.6 copy-start.22
  101.9 2.9 copy-start.16
  101.9 3.1 copy-start.7
  101.9 3.1 copy-start.20
  141.4 18.5 %copy-start.4 = (bf16[1,6,64,768]{3,2,1,0:T(8,128)(2,1)S(1)}, bf16[1,6,64,768]{3,2,1,0:T(8,128)(2,1)}, u32[]{:S(2)}) copy-start(bf16[1,6,64,768]{3,2,1,0:T(8,128)(2,1)} %get-tuple-element.66) | copy-start | bytes 1769476
  147.1 13.7 %copy-start.3 = (bf16[1,6,64,768]{3,2,1,0:T(8,128)(2,1)S(1)}, bf16[1,6,64,768]{3,2,1,0:T(8,128)(2,1)}, u32[]{:S(2)}) copy-start(bf16[1,6,64,768]{3,2,1,0:T(8,128)(2,1)} %get-tuple-element.63) | copy-start | bytes 1769476
  147.1 13.7 %copy-start.9 = (f32[24,768]{1,0:T(8,128)S(1)}, f32[24,768]{1,0:T(8,128)}, u32[]{:S(2)}) copy-start(f32[24,768]{1,0:T(8,128)} %get-tuple-element.116) | copy-start | bytes 221188
  148.9 13.1 %copy-start.23 = (f32[1,4,768]{2,0,1:T(1,128)S(1)}, f32[1,4,768]{2,0,1:T(1,128)}, u32[]{:S(2)}) copy-start(f32[1,4,768]{2,0,1:T(1,128)} %get-tuple-element.105) | copy-start | bytes 36868
  148.9 13.1 %copy-start.29 = (f32[768]{0:T(1024)S(1)}, f32[768]{0:T(1024)}, u32[]{:S(2)}) copy-start(f32[768]{0:T(1024)} %get-tuple-element.21) | copy-start | bytes 9220
  148.9 13.1 %copy-start.30 = (f32[768]{0:T(1024)S(1)}, f32[768]{0:T(1024)}, u32[]{:S(2)}) copy-start(f32[768]{0:T(1024)} %get-tuple-element.22) | copy-start | bytes 9220
  148.9 13.2 %copy-start.31 = (f32[768]{0:T(1024)S(1)}, f32[768]{0:T(1024)}, u32[]{:S(2)}) copy-start(f32[768]{0:T(1024)} %get-tuple-element.36) | copy-start | bytes 9220
  162.1 6.1 %copy-start.24 = (f32[2,768]{1,0:T(2,128)S(1)}, f32[2,768]{1,0:T(2,128)}, u32[]{:S(2)}) copy-start(f32[2,768]{1,0:T(2,128)} %param.32) | copy-start | bytes 18436
  162.1 6.2 %copy-start.12 = (bf16[768,384]{1,0:T(8,128)(2,1)S(1)}, bf16[768,384]{1,0:T(8,128)(2,1)}, u32[]{:S(2)}) copy-start(bf16[768,384]{1,0:T(8,128)(2,1)} %param.33) | copy-start | bytes 1769476
  162.1 6.2 %copy-start.26 = (s32[128]{0:T(128)S(1)}, s32[128]{0:T(128)}, u32[]{:S(2)}) copy-start(s32[128]{0:T(128)} %copy-done.25) | copy-start | bytes 1540
  167.9 15.4 %copy-start.36 = (bf16[384]{0:T(512)(128)(2,1)S(1)}, bf16[384]{0:T(512)(128)(2,1)}, u32[]{:S(2)}) copy-start(bf16[384]{0:T(512)(128)(2,1)} %param.34) | copy-start | bytes 2308
  167.9 15.4 %copy-start.15 = (bf16[192,384]{1,0:T(8,128)(2,1)S(1)}, bf16[192,384]{1,0:T(8,128)(2,1)}, u32[]{:S(2)}) copy-start(bf16[192,384]{1,0:T(8,128)(2,1)} %param.24) | copy-start | bytes 442372
  168.0 15.4 %copy-start.28 = (s32[192]{0:T(256)S(1)}, s32[192]{0:T(256)}, u32[]{:S(2)}) copy-start(s32[192]{0:T(256)} %copy-done.27) | copy-start | bytes 2308
  168.0 15.4 %copy-start.33 = (pred[192]{0:T(512)(128)(4,1)S(1)}, pred[192]{0:T(512)(128)(4,1)}, u32[]{:S(2)}) copy-start(pred[192]{0:T(512)(128)(4,1)} %get-tuple-element.60) | copy-start | bytes 580
  168.0 16.0 %copy-start.19 = (f32[2,12,384]{2,0,1:T(2,128)S(1)}, f32[2,12,384]{2,0,1:T(2,128)}, u32[]{:S(2)}) copy-start(f32[2,12,384]{2,0,1:T(2,128)} %param.35) | copy-start | bytes 110596
  168.2 15.9 %copy-start.5 = (bf16[2,384,3,6,64]{1,4,3,2,0:T(8,128)(2,1)S(1)}, bf16[2,384,3,6,64]{1,4,3,2,0:T(8,128)(2,1)}, u32[]{:S(2)}) copy-start(bf16[2,384,3,6,64]{1,4,3,2,0:T(8,128)(2,1)} %param.36) | copy-start | bytes 5308420
  335.0 25.6 %copy-start.13 = (bf16[2,6,64,384]{3,2,1,0:T(8,128)(2,1)S(1)}, bf16[2,6,64,384]{3,2,1,0:T(8,128)(2,1)}, u32[]{:S(2)}) copy-start(bf16[2,6,64,384]{3,2,1,0:T(8,128)(2,1)} %param.37) | copy-start | bytes 1769476
  362.3 5.2 copy-start.2
  515.7 25.6 %copy-start.11 = (bf16[1,3,64,384]{3,2,1,0:T(8,128)(2,1)S(1)}, bf16[1,3,64,384]{3,2,1,0:T(8,128)(2,1)}, u32[]{:S(2)}) copy-start(bf16[1,3,64,384]{3,2,1,0:T(8,128)(2,1)} %get-tuple-element.76) | copy-start | bytes 442372
  515.7 26.7 %copy-start.10 = (bf16[1,3,64,384]{3,2,1,0:T(8,128)(2,1)S(1)}, bf16[1,3,64,384]{3,2,1,0:T(8,128)(2,1)}, u32[]{:S(2)}) copy-start(bf16[1,3,64,384]{3,2,1,0:T(8,128)(2,1)} %get-tuple-element.73) | copy-start | bytes 442372
  543.9 5.2 copy-start.32
  549.1 3.0 copy-start.1
  (6 other events, 7.0 us)

commit v2 on v1

--- a/solution.py
+++ b/solution.py
@@ -16,6 +16,9 @@
 MESH = pl.DeviceIdType.MESH
 RING = (1, 3, 2)
 VMEM_LIMIT = 60 * 1024 * 1024
+LOG2E = 1.4426950408889634
+SAFE_SCORE = 60.0
+SAFE_VALUE = 1e7
 
 
 def position():
@@ -139,55 +142,118 @@
     )(a, b, q)
 
 
-def flash_kernel(heads, key_block, steps, q_ref, k_ref, vt_ref, out_ref, acc_ref, stat_ref):
+def flash_kernel(heads, key_block, steps, v_lane, q_ref, k_ref, v_ref, out_ref, acc_ref, stat_ref, vt_ref, norm_ref):
     width = heads * HEAD
+    lanes = q_ref.shape[-1]
+    pairs = -(-heads // 2) * 128
+    scale = HEAD ** -0.5
+    v_base = v_lane % 128
+    v_first = v_lane - v_base
+
+    @pl.when(pl.program_id(0) == 0)
+    def prepare():
+        rows = lax.broadcasted_iota(jnp.int32, (pairs, 128), 0)
+        cols = lax.broadcasted_iota(jnp.int32, (pairs, 128), 1)
+        picks = ((rows // HEAD == cols) & (cols < heads)).astype(jnp.bfloat16)
+        norm_ref[...] = jnp.zeros_like(norm_ref)
+
+        def turn_block(i, _):
+            at = pl.multiple_of(i * key_block, key_block)
+            values = v_ref[pl.ds(at, key_block), v_first:v_first + vt_ref.shape[0]]
+            vt_ref[:, pl.ds(at, key_block)] = values.T
+            k_rows = k_ref[pl.ds(at, key_block), :pairs].astype(jnp.float32)
+            sums = jnp.dot((k_rows * k_rows).astype(jnp.bfloat16), picks, preferred_element_type=jnp.float32)
+            norm_ref[0] = jnp.maximum(norm_ref[0], jnp.max(sums.reshape(key_block // 8, 8, 128), axis=0))
+            sizes = jnp.abs(values.astype(jnp.float32))
+            for j in range(vt_ref.shape[0] // 128):
+                part = sizes[:, j * 128:(j + 1) * 128].reshape(key_block // 8, 8, 128)
+                norm_ref[1] = jnp.maximum(norm_ref[1], jnp.max(part, axis=0))
+            return 0
+
+        lax.fori_loop(0, steps, turn_block, 0)
+
     acc_ref[...] = jnp.zeros_like(acc_ref)
-    lanes = q_ref.shape[-1]
+    stat_ref[...] = jnp.zeros_like(stat_ref)
+    k_norm = jnp.max(norm_ref[0], axis=0, keepdims=True)
+    lane = lax.broadcasted_iota(jnp.int32, (1, 128), 1)
+    bound = jnp.zeros((1, 128), jnp.float32)
     for h in range(heads):
-        stat_ref[h] = jnp.full((8, lanes), -jnp.inf, jnp.float32)
-        stat_ref[heads + h] = jnp.zeros((8, lanes), jnp.float32)
-
-    def step(i, _):
-        at = pl.multiple_of(i * key_block, key_block)
+        q_rows = q_ref[h].astype(jnp.float32)
+        q_norm = jnp.max(jnp.sum(q_rows * q_rows, axis=0, keepdims=True), axis=1, keepdims=True)
+        bound = jnp.where(lane == h, q_norm * k_norm, bound)
+    limit = (SAFE_SCORE / scale) ** 2 / 1.05
+    safe = (jnp.max(bound) <= limit) & (jnp.max(norm_ref[1]) <= SAFE_VALUE)
+
+    def scores_of(at, size, h):
+        k_rows = k_ref[pl.ds(at, size), (h // 2) * 128:(h // 2 + 1) * 128]
+        return jnp.dot(k_rows, q_ref[h], preferred_element_type=jnp.float32)
+
+    def weighted(at, size, h, weights):
+        values = vt_ref[v_base + h * HEAD:v_base + (h + 1) * HEAD, pl.ds(at, size)]
+        return jnp.dot(values, weights.astype(jnp.bfloat16), preferred_element_type=jnp.float32)
+
+    @pl.when(safe)
+    def plain():
+        def step(i, _):
+            at = pl.multiple_of(i * key_block, key_block)
+            for h in range(heads):
+                weights = jnp.exp2(scores_of(at, key_block, h) * (scale * LOG2E))
+                stat_ref[heads + h] += jnp.sum(weights.reshape(key_block // 8, 8, lanes), axis=0)
+                acc_ref[h * HEAD:(h + 1) * HEAD] += weighted(at, key_block, h, weights)
+            return 0
+
+        lax.fori_loop(0, steps, step, 0)
         for h in range(heads):
-            k_rows = k_ref[pl.ds(at, key_block), (h // 2) * 128:(h // 2 + 1) * 128]
-            scores = jnp.dot(k_rows, q_ref[h], preferred_element_type=jnp.float32)
-            old = stat_ref[h, 0:1]
-            new = jnp.maximum(old, jnp.max(scores, axis=0, keepdims=True))
-            weights = jnp.exp(scores - new)
-            fade = jnp.exp(old - new)
-            stat_ref[h, 0:1] = new
-            stat_ref[heads + h, 0:1] = stat_ref[heads + h, 0:1] * fade + jnp.sum(weights, axis=0, keepdims=True)
-            part = jnp.dot(vt_ref[h * HEAD:(h + 1) * HEAD, pl.ds(at, key_block)], weights.astype(jnp.bfloat16), preferred_element_type=jnp.float32)
-            acc_ref[h * HEAD:(h + 1) * HEAD] = acc_ref[h * HEAD:(h + 1) * HEAD] * fade + part
-        return 0
-
-    lax.fori_loop(0, steps, step, 0)
-    for h in range(heads):
-        acc_ref[width + h:width + h + 1] = stat_ref[h, 0:1]
-        acc_ref[width + heads + h:width + heads + h + 1] = stat_ref[heads + h, 0:1]
+            acc_ref[width + heads + h:width + heads + h + 1] = jnp.sum(stat_ref[heads + h], axis=0, keepdims=True)
+
+    @pl.when(jnp.logical_not(safe))
+    def shifted():
+        size = 256
+        for h in range(heads):
+            stat_ref[h] = jnp.full((8, lanes), -jnp.inf, jnp.float32)
+
+        def step(i, _):
+            at = pl.multiple_of(i * size, size)
+            for h in range(heads):
+                scores = scores_of(at, size, h) * scale
+                old = stat_ref[h, 0:1]
+                new = jnp.maximum(old, jnp.max(scores, axis=0, keepdims=True))
+                weights = jnp.exp(scores - new)
+                fade = jnp.exp(old - new)
+                stat_ref[h, 0:1] = new
+                stat_ref[heads + h, 0:1] = stat_ref[heads + h, 0:1] * fade + jnp.sum(weights, axis=0, keepdims=True)
+                acc_ref[h * HEAD:(h + 1) * HEAD] = acc_ref[h * HEAD:(h + 1) * HEAD] * fade + weighted(at, size, h, weights)
+            return 0
+
+        lax.fori_loop(0, steps * key_block // size, step, 0)
+        for h in range(heads):
+            acc_ref[width + h:width + h + 1] = stat_ref[h, 0:1]
+            acc_ref[width + heads + h:width + heads + h + 1] = stat_ref[heads + h, 0:1]
+
     out_ref[...] = acc_ref[...].T
 
 
-def flash(q, k, vt, key_block):
+def flash(q, k, v, v_lane, key_block, block):
     heads, _, queries = q.shape
     keys, lanes = k.shape
     out_lanes = -(-(heads * HEAD + 2 * heads) // 128) * 128
-    block = 256
+    v_rows = v.shape[1] - v_lane // 128 * 128
+    whole = pl.BlockSpec((keys, lanes), lambda i: (0, 0))
     return pl.pallas_call(
-        functools.partial(flash_kernel, heads, key_block, keys // key_block),
+        functools.partial(flash_kernel, heads, key_block, keys // key_block, v_lane),
         grid=(queries // block,),
         out_shape=jax.ShapeDtypeStruct((queries, out_lanes), jnp.float32),
-        in_specs=[
-            pl.BlockSpec((heads, 128, block), lambda i: (0, 0, i)),
-            pl.BlockSpec((keys, lanes), lambda i: (0, 0)),
-            pl.BlockSpec((heads * HEAD, keys), lambda i: (0, 0)),
+        in_specs=[pl.BlockSpec((heads, 128, block), lambda i: (0, 0, i)), whole, whole],
+        out_specs=pl.BlockSpec((block, out_lanes), lambda i: (i, 0)),
+        scratch_shapes=[
+            pltpu.VMEM((out_lanes, block), jnp.float32),
+            pltpu.VMEM((2 * heads, 8, block), jnp.float32),
+            pltpu.VMEM((v_rows, keys), jnp.bfloat16),
+            pltpu.VMEM((2, 8, 128), jnp.float32),
         ],
-        out_specs=pl.BlockSpec((block, out_lanes), lambda i: (i, 0)),
-        scratch_shapes=[pltpu.VMEM((out_lanes, block), jnp.float32), pltpu.VMEM((2 * heads, 8, block), jnp.float32)],
         compiler_params=pltpu.CompilerParams(vmem_limit_bytes=VMEM_LIMIT),
         name="flash",
-    )(q, k, vt)
+    )(q, k, v)
 
 
 def combine_kernel(heads, part_ref, out_ref, got_ref, send_sem, recv_sem):
@@ -275,35 +341,26 @@
     lax.fori_loop(1, REGIONS, signal, 0)
     pl.semaphore_wait(barrier, REGIONS - 1)
 
-    def copy_to(peer, slot):
-        return pltpu.make_async_remote_copy(
+    def start(d, _):
+        peer = lax.rem(me + d, REGIONS)
+        pltpu.make_async_remote_copy(
             src_ref=src_ref if spread else src_ref.at[peer],
-            dst_ref=dst_ref.at[slot],
-            send_sem=send_sem.at[peer],
-            recv_sem=recv_sem.at[slot],
+            dst_ref=dst_ref.at[me],
+            send_sem=send_sem,
+            recv_sem=recv_sem,
             device_id={"time": t, "region": peer},
             device_id_type=MESH,
-        )
-
-    def start(d, _):
-        copy_to(lax.rem(me + d, REGIONS), me).start()
+        ).start()
         return 0
 
     lax.fori_loop(1, REGIONS, start, 0)
+    rest = dst_ref.at[pl.ds(0, REGIONS - 1)]
+    everything = pltpu.make_async_remote_copy(
+        src_ref=rest, dst_ref=rest, send_sem=send_sem, recv_sem=recv_sem, device_id={"time": t, "region": me}, device_id_type=MESH
+    )
+    everything.wait_recv()
+    everything.wait_send()
     dst_ref[me] = src_ref[...] if spread else src_ref[me]
-
-    def finish(d, _):
-        peer = lax.rem(me + d, REGIONS)
-        copy_to(peer, peer).wait_recv()
-        return 0
-
-    lax.fori_loop(1, REGIONS, finish, 0)
-
-    def drain(d, _):
-        copy_to(lax.rem(me + d, REGIONS), me).wait_send()
-        return 0
-
-    lax.fori_loop(1, REGIONS, drain, 0)
 
 
 def exchange(rows, spread, collective_id):
@@ -314,7 +371,7 @@
         out_shape=jax.ShapeDtypeStruct((REGIONS,) + block, rows.dtype),
         in_specs=[vmem],
         out_specs=vmem,
-        scratch_shapes=[pltpu.SemaphoreType.DMA((REGIONS,)), pltpu.SemaphoreType.DMA((REGIONS,))],
+        scratch_shapes=[pltpu.SemaphoreType.DMA, pltpu.SemaphoreType.DMA],
         compiler_params=pltpu.CompilerParams(collective_id=collective_id, has_side_effects=True),
         name="exchange",
     )(rows)
@@ -328,7 +385,7 @@
     return centered * lax.rsqrt(variance + LN_EPS) * ln_gain + ln_shift
 
 
-def run_block(hidden, vec_rows, w_qkv, w_o, w_one, w_two, key_block, collective_id):
+def run_block(hidden, vec_rows, w_qkv, w_o, w_one, w_two, collective_id):
     tokens, width = hidden.shape
     heads = w_qkv.shape[2] // 2
     half = heads * HEAD
@@ -341,7 +398,7 @@
     def halves(part):
         return jnp.stack([projected[:, part * width + c * half:part * width + (c + 1) * half] for c in range(2)])
 
-    q, k, v = halves(0) * jnp.bfloat16(HEAD ** -0.5), halves(1), halves(2)
+    q, k, v = halves(0), halves(1), halves(2)
     if half % 128 == 0:
         a, b = k, v
     else:
@@ -349,21 +406,21 @@
         a, b = both[:, :tokens // 2], both[:, tokens // 2:]
     kv_all, q_all = gather(a, b, q, collective_id)
     if half % 128 == 0:
-        keys = kv_all[0].reshape(-1, half)
-        values_t = kv_all[1].reshape(-1, half).T
+        keys, values, v_lane = kv_all[0].reshape(-1, half), kv_all[1].reshape(-1, half), 0
     else:
-        keys = kv_all.reshape(-1, 2 * half)
-        values_t = keys[:, half:].T
+        keys = values = kv_all.reshape(-1, 2 * half)
+        v_lane = half
     count = ROW * tokens
     queries = q_all.reshape(count, heads, HEAD).transpose(1, 2, 0)
-    padded = -(-count // 256) * 256
+    block = 512 if count % 512 == 0 else 256
+    padded = -(-count // block) * block
     rows = jnp.arange(heads) % 2
     zeros = jnp.zeros_like(queries)
     even = jnp.concatenate([queries, zeros], axis=1)
     odd = jnp.concatenate([zeros, queries], axis=1)
     queries = jnp.where((rows == 0)[:, None, None], even, odd)
     queries = jnp.pad(queries, ((0, 0), (0, 0), (0, padded - count)))
-    parts = flash(queries, keys, values_t, key_block)[:count].reshape(ROW, tokens, -1)
+    parts = flash(queries, keys, values, v_lane, 768, block)[:count].reshape(ROW, tokens, -1)
     attended = combine(parts, heads, collective_id + 1)
     w_o = w_o.reshape(2, half, width)
     mixed = sum(jnp.dot(attended[c], w_o[c], preferred_element_type=jnp.float32) for c in range(2))
@@ -402,14 +459,14 @@
         sent = one_hot_rows(deal, embedded).reshape(REGIONS, 2, -1)
         hidden = one_hot_rows(pack, exchange(sent, False, 2).reshape(2 * REGIONS, -1))
         for layer in range(enc_vec.shape[0]):
-            hidden = run_block(hidden, enc_vec[layer], enc_wqkv[layer], enc_wo[layer], enc_w1[layer], enc_w2[layer], 768, 4 + 2 * layer)
+            hidden = run_block(hidden, enc_vec[layer], enc_wqkv[layer], enc_wo[layer], enc_w1[layer], enc_w2[layer], 4 + 2 * layer)
         latent = jnp.dot(layer_norm(hidden, enc_final[0], enc_final[1]).astype(jnp.bfloat16), w_dec_in, preferred_element_type=jnp.float32).astype(jnp.bfloat16)
         back = one_hot_rows(pack.T, latent).reshape(REGIONS, 2, -1)
         returned = exchange(back, False, 3).reshape(2 * REGIONS, -1)
         placed = jnp.dot(deal.T.astype(jnp.bfloat16), returned, preferred_element_type=jnp.float32)
         hidden = (jnp.where(vis_mask[:, None] == 1, placed, mask_token.astype(jnp.float32)) + dec_pos.astype(jnp.float32)).astype(jnp.bfloat16)
         for layer in range(dec_vec.shape[0]):
-            hidden = run_block(hidden, dec_vec[layer], dec_wqkv[layer], dec_wo[layer], dec_w1[layer], dec_w2[layer], 512, 8 + 2 * layer)
+            hidden = run_block(hidden, dec_vec[layer], dec_wqkv[layer], dec_wo[layer], dec_w1[layer], dec_w2[layer], 8 + 2 * layer)
         return jnp.dot(layer_norm(hidden, dec_final[0], dec_final[1]).astype(jnp.bfloat16), w_out, preferred_element_type=jnp.float32)
 
     token_rows = P(TOKEN_AXES, None)

time: 556 us -> 422 us (0.76)
  Pallas kernels: 438 us -> 318 us
  local copies, waits for them, and re-layouts: 56.6 us -> 38.6 us
    pallas_call x4, Pallas kernels: 203 us -> 88.5 us  [flash(): pl.pallas_call(functools.partial(flash_kernel, heads, key_block, keys //...]
    slice x6 -> x4, local copies, waits for them, and re-layouts: 15.4 us -> 5.84 us  [the longest x2 3.59 us: run_block(): flash(queries, keys, values, v_lane, 768, block)[:count]]
    pallas_call x3, Pallas kernels: 44.4 us -> 38.1 us  [exchange(): pl.pallas_call(functools.partial(exchange_kernel, spread), out_shape=jax....]
where the time goes in v2:
time: 422 us; the launch traced here: 414 us
  Pallas kernels  318 us (75%)
  local copies, waits for them, and re-layouts  38.6 us (9%)
  matrix products  37.9 us (9%)
  other arithmetic  18.4 us (4%)
    pallas_call x4, Pallas kernels, gather(): pl.pallas_call(gather_kernel, out_shape=(jax.ShapeDtypeStruct((2, PLANE,...  118 us
    pallas_call x4, Pallas kernels, flash(): pl.pallas_call(functools.partial(flash_kernel, heads, key_block, keys //...  88.5 us
    pallas_call x4, Pallas kernels, combine(): pl.pallas_call(functools.partial(combine_kernel, heads), out_shape=jax.Sh...  73.3 us
    pallas_call x3, Pallas kernels, exchange(): pl.pallas_call(functools.partial(exchange_kernel, spread), out_shape=jax....  38.1 us
    dot_general x4, matrix products, run_block(): jnp.dot(mlp_hidden, w_two, preferred_element_type=jnp.float32)  22.7 us

profile of v2, /device:TPU:1, one launch (start us, length us, event | category | flops | bytes accessed | tf_op | source)
XLA Modules:
  0.0 413.8 jit_solution(589467304776821611)
XLA Ops:
  5.0 15.5 %exchange.3 = s32[64,8,128]{2,1,0:T(8,128)} custom-call(s32[8,128]{1,0:T(8,128)} %broadcast_in_dim.77.src_ref), custom_call_target="tpu_custom_call" | custom-call | tf_op jit(solution)/shard_map/exchange/pallas_call | solution.py:369
  20.5 2.2 slice_reduce_fusion
  24.8 1.8 fusion.376
  26.6 2.0 convolution_convert_fusion
  29.3 11.7 %exchange.4 = bf16[64,2,768]{2,1,0:T(2,128)(2,1)} custom-call(bf16[64,2,768]{2,1,0:T(2,128)(2,1)} %reshape.359.src_ref), custom_call_target="tpu_custom_call" | custom-call | tf_op jit(solution)/shard_map/exchange/pallas_call | solution.py:369
  42.6 3.6 fusion.505
  48.6 20.4 %gather_kv.4 = (bf16[2,32,24,384]{3,2,1,0:T(8,128)(2,1)}, bf16[8,24,384]{2,1,0:T(8,128)(2,1)}) custom-call(bf16[2,24,384]{2,1,0:T(8,128)(2,1)} %get-tuple-element.131.a_ref, bf16[2,24,384]{2,1,0:T(8,128)(2,1)} %get-tuple-element.132.b_ref, bf16[2,24,384]{2,1,0:T(8,128)(2,1)} %pad_maximum_fusion.4.q_ref), custom_call_target="tpu_custom_call" | custom-call | tf_op jit(solution)/shard_map/gather_kv/pallas_call | solution.py:124
  69.0 1.9 reshape.362
  70.9 1.9 copy.30
  76.0 5.3 %flash.4 = f32[256,512]{1,0:T(8,128)} custom-call(bf16[6,128,256]{2,1,0:T(8,128)(2,1)} %pad.15.q_ref, bf16[768,384]{1,0:T(8,128)(2,1)} %bitcast.253, bf16[768,384]{1,0:T(8,128)(2,1)} %bitcast.252), custom_call_target="tpu_custom_call" | custom-call | tf_op jit(solution)/shard_map/flash/pallas_call | solution.py:242
  81.3 1.8 slice.520
  83.1 10.9 %combine.4 = bf16[2,24,384]{2,1,0:T(8,128)(2,1)} custom-call(f32[8,24,512]{2,1,0:T(8,128)} %bitcast.258), custom_call_target="tpu_custom_call" | custom-call | tf_op jit(solution)/shard_map/combine/pallas_call | solution.py:317
  94.0 2.9 fusion.506
  100.2 7.0 %fusion.516 = (f32[24]{0:T(128)}, f32[24,768]{1,0:T(8,128)}) fusion(f32[768]{0:T(1024)} %get-tuple-element.28, f32[24,768]{1,0:T(8,128)} %copy-done.13, bf16[2,3072,768]{2,1,0:T(8,128)(2,1)} %param.31, bf16[2,768,3072]{2,1,0:T(8,128)(2,1)} %param.30, f32[3072]{0:T(1024)} %bitcast.267, f32[768]{0:T(1024)} %get-tuple-element.29, f32[768]{0:T(1024)} %get-tuple-element.30, ...), kind=kOutput, calls=%fused_computation.642 | convolution fusion | flops 231542752 | bytes 9684064 | tf_op jit(solution)/shard_map/dot_general | solution.py:430
  109.0 2.0 fusion.19
  112.8 16.0 %gather_kv.5 = (bf16[2,32,24,384]{3,2,1,0:T(8,128)(2,1)}, bf16[8,24,384]{2,1,0:T(8,128)(2,1)}) custom-call(bf16[2,24,384]{2,1,0:T(8,128)(2,1)} %pad_maximum_fusion.5.a_ref, bf16[2,24,384]{2,1,0:T(8,128)(2,1)} %pad_maximum_fusion.6.b_ref, bf16[2,24,384]{2,1,0:T(8,128)(2,1)} %pad_maximum_fusion.7.q_ref), custom_call_target="tpu_custom_call" | custom-call | tf_op jit(solution)/shard_map/gather_kv/pallas_call | solution.py:124
  132.4 5.4 %flash.5 = f32[256,512]{1,0:T(8,128)} custom-call(bf16[6,128,256]{2,1,0:T(8,128)(2,1)} %pad.16.q_ref, bf16[768,384]{1,0:T(8,128)(2,1)} %bitcast.255, bf16[768,384]{1,0:T(8,128)(2,1)} %bitcast.254), custom_call_target="tpu_custom_call" | custom-call | tf_op jit(solution)/shard_map/flash/pallas_call | solution.py:242
  137.8 1.8 slice.527
  139.7 11.1 %combine.5 = bf16[2,24,384]{2,1,0:T(8,128)(2,1)} custom-call(f32[8,24,512]{2,1,0:T(8,128)} %bitcast.259), custom_call_target="tpu_custom_call" | custom-call | tf_op jit(solution)/shard_map/combine/pallas_call | solution.py:317
  153.0 5.8 %fusion.520 = (f32[24]{0:T(128)S(1)}, f32[24,768]{1,0:T(8,128)S(1)}) fusion(f32[768]{0:T(1024)S(1)} %copy-done.29, f32[24,768]{1,0:T(8,128)S(1)} %get-tuple-element.118, bf16[2,3072,768]{2,1,0:T(8,128)(2,1)} %param.31, bf16[2,768,3072]{2,1,0:T(8,128)(2,1)} %param.30, f32[3072]{0:T(1024)S(1)} %bitcast.266, f32[768]{0:T(1024)S(1)} %copy-done.28, ...), kind=kOutput, calls=%fused_computation.644 | convolution fusion | flops 231542752 | bytes 9684064 | tf_op jit(solution)/shard_map/dot_general | solution.py:430
  160.3 10.8 %exchange.5 = bf16[64,2,384]{2,1,0:T(2,128)(2,1)} custom-call(bf16[64,2,384]{2,1,0:T(2,128)(2,1)} %reshape.367.src_ref), custom_call_target="tpu_custom_call" | custom-call | tf_op jit(solution)/shard_map/exchange/pallas_call | solution.py:369
  175.4 41.2 %gather_kv.6 = (bf16[2,32,96,384]{3,2,1,0:T(8,128)(2,1)}, bf16[8,192,192]{2,1,0:T(8,128)(2,1)}) custom-call(bf16[2,96,384]{2,1,0:T(8,128)(2,1)} %get-tuple-element.92.a_ref, bf16[2,96,384]{2,1,0:T(8,128)(2,1)} %get-tuple-element.91.b_ref, bf16[2,192,192]{2,1,0:T(8,128)(2,1)} %pad_maximum_fusion.q_ref), custom_call_target="tpu_custom_call" | custom-call | tf_op jit(solution)/shard_map/gather_kv/pallas_call | solution.py:124
  216.6 1.8 copy.32
  220.4 38.9 %flash.6 = f32[1536,256]{1,0:T(8,128)} custom-call(bf16[3,128,1536]{2,1,0:T(8,128)(2,1)} %pad_select_fusion.1.q_ref, bf16[6144,384]{1,0:T(8,128)(2,1)} %bitcast.238, bf16[6144,384]{1,0:T(8,128)(2,1)} %bitcast.239), custom_call_target="tpu_custom_call" | custom-call | tf_op jit(solution)/shard_map/flash/pallas_call | solution.py:242
  259.3 25.7 %combine.6 = bf16[2,192,256]{2,1,0:T(8,128)(2,1)} custom-call(f32[8,192,256]{2,1,0:T(8,128)} %bitcast.244), custom_call_target="tpu_custom_call" | custom-call | tf_op jit(solution)/shard_map/combine/pallas_call | solution.py:317
  286.7 4.9 %fusion.525 = (f32[192]{0:T(256)S(1)}, f32[192,384]{1,0:T(8,128)S(1)}) fusion(f32[384]{0:T(512)S(1)} %get-tuple-element.44, f32[192,384]{1,0:T(8,128)S(1)} %get-tuple-element.124, bf16[2,1536,384]{2,1,0:T(8,128)(2,1)} %param.39, bf16[2,384,1536]{2,1,0:T(8,128)(2,1)} %param.38, f32[1536]{0:T(1024)S(1)} %add.541, f32[384]{0:T(512)S(1)} %get-tuple-element.45, ...), kind=kOutput, calls=%fused_computation.647 | convolution fusion | flops 473186112 | bytes 3261184 | tf_op jit(solution)/shard_map/dot_general | solution.py:430
  294.2 40.1 %gather_kv.7 = (bf16[2,32,96,384]{3,2,1,0:T(8,128)(2,1)}, bf16[8,192,192]{2,1,0:T(8,128)(2,1)}) custom-call(bf16[2,96,384]{2,1,0:T(8,128)(2,1)} %get-tuple-element.90.a_ref, bf16[2,96,384]{2,1,0:T(8,128)(2,1)} %get-tuple-element.89.b_ref, bf16[2,192,192]{2,1,0:T(8,128)(2,1)} %pad_maximum_fusion.1.q_ref), custom_call_target="tpu_custom_call" | custom-call | tf_op jit(solution)/shard_map/gather_kv/pallas_call | solution.py:124
  334.3 1.8 copy.33
  338.1 38.9 %flash.7 = f32[1536,256]{1,0:T(8,128)} custom-call(bf16[3,128,1536]{2,1,0:T(8,128)(2,1)} %pad_select_fusion.q_ref, bf16[6144,384]{1,0:T(8,128)(2,1)} %bitcast.240, bf16[6144,384]{1,0:T(8,128)(2,1)} %bitcast.241), custom_call_target="tpu_custom_call" | custom-call | tf_op jit(solution)/shard_map/flash/pallas_call | solution.py:242
  377.0 25.6 %combine.7 = bf16[2,192,256]{2,1,0:T(8,128)(2,1)} custom-call(f32[8,192,256]{2,1,0:T(8,128)} %bitcast.245), custom_call_target="tpu_custom_call" | custom-call | tf_op jit(solution)/shard_map/combine/pallas_call | solution.py:317
  405.2 4.9 %fusion.529 = (f32[192]{0:T(256)S(1)}, f32[192,384]{1,0:T(8,128)S(1)}) fusion(f32[384]{0:T(512)S(1)} %get-tuple-element.52, f32[192,384]{1,0:T(8,128)S(1)} %get-tuple-element.128, bf16[2,1536,384]{2,1,0:T(8,128)(2,1)} %param.39, bf16[2,384,1536]{2,1,0:T(8,128)(2,1)} %param.38, f32[1536]{0:T(1024)S(1)} %add.563, f32[384]{0:T(512)S(1)} %get-tuple-element.38, ...), kind=kOutput, calls=%fused_computation.649 | convolution fusion | flops 473186112 | bytes 3261184 | tf_op jit(solution)/shard_map/dot_general | solution.py:430
  410.4 3.0 fusion.222
  (174 shorter events, 43.9 us)
Async XLA Ops:
  0.0 26.6 %copy-start = (bf16[1536,768]{1,0:T(8,128)(2,1)S(1)}, bf16[1536,768]{1,0:T(8,128)(2,1)}, u32[]{:S(2)}) copy-start(bf16[1536,768]{1,0:T(8,128)(2,1)} %param.25) | copy-start | bytes 7077892
  23.3 18.8 %copy-start.23 = (s32[128]{0:T(128)}, s32[128]{0:T(128)S(1)}, u32[]{:S(2)}) copy-start(s32[128]{0:T(128)S(1)} %compare_select_fusion.6) | copy-start | bytes 1540
  42.4 3.8 copy-start.7
  42.6 3.6 copy-start.16
  42.6 3.6 copy-start.19
  42.6 3.6 copy-start.20
  72.8 2.1 copy-start.6
  72.8 2.1 copy-start.32
  93.9 2.9 copy-start.15
  94.0 3.1 copy-start.8
  94.0 3.1 copy-start.18
  110.9 19.4 %copy-start.33 = (pred[6]{0:T(512)(128)(4,1)S(1)}, pred[6]{0:T(512)(128)(4,1)}, u32[]{:S(2)}) copy-start(pred[6]{0:T(512)(128)(4,1)} %copy-done.32) | copy-start | bytes 22
  128.8 2.5 copy-start.5
  132.4 18.3 %copy-start.3 = (bf16[1,6,64,768]{3,2,1,0:T(8,128)(2,1)S(1)}, bf16[1,6,64,768]{3,2,1,0:T(8,128)(2,1)}, u32[]{:S(2)}) copy-start(bf16[1,6,64,768]{3,2,1,0:T(8,128)(2,1)} %get-tuple-element.66) | copy-start | bytes 1769476
  137.8 13.9 %copy-start.2 = (bf16[1,6,64,768]{3,2,1,0:T(8,128)(2,1)S(1)}, bf16[1,6,64,768]{3,2,1,0:T(8,128)(2,1)}, u32[]{:S(2)}) copy-start(bf16[1,6,64,768]{3,2,1,0:T(8,128)(2,1)} %get-tuple-element.63) | copy-start | bytes 1769476
  137.8 13.9 %copy-start.10 = (f32[24,768]{1,0:T(8,128)S(1)}, f32[24,768]{1,0:T(8,128)}, u32[]{:S(2)}) copy-start(f32[24,768]{1,0:T(8,128)} %get-tuple-element.116) | copy-start | bytes 221188
  139.7 13.3 %copy-start.21 = (f32[1,4,768]{2,0,1:T(1,128)S(1)}, f32[1,4,768]{2,0,1:T(1,128)}, u32[]{:S(2)}) copy-start(f32[1,4,768]{2,0,1:T(1,128)} %get-tuple-element.105) | copy-start | bytes 36868
  139.7 13.3 %copy-start.27 = (f32[768]{0:T(1024)S(1)}, f32[768]{0:T(1024)}, u32[]{:S(2)}) copy-start(f32[768]{0:T(1024)} %get-tuple-element.21) | copy-start | bytes 9220
  139.7 13.3 %copy-start.28 = (f32[768]{0:T(1024)S(1)}, f32[768]{0:T(1024)}, u32[]{:S(2)}) copy-start(f32[768]{0:T(1024)} %get-tuple-element.22) | copy-start | bytes 9220
  139.7 13.3 %copy-start.29 = (f32[768]{0:T(1024)S(1)}, f32[768]{0:T(1024)}, u32[]{:S(2)}) copy-start(f32[768]{0:T(1024)} %get-tuple-element.36) | copy-start | bytes 9220
  153.0 6.1 %copy-start.22 = (f32[2,768]{1,0:T(2,128)S(1)}, f32[2,768]{1,0:T(2,128)}, u32[]{:S(2)}) copy-start(f32[2,768]{1,0:T(2,128)} %param.32) | copy-start | bytes 18436
  153.0 6.2 %copy-start.11 = (bf16[768,384]{1,0:T(8,128)(2,1)S(1)}, bf16[768,384]{1,0:T(8,128)(2,1)}, u32[]{:S(2)}) copy-start(bf16[768,384]{1,0:T(8,128)(2,1)} %param.33) | copy-start | bytes 1769476
  153.0 6.2 %copy-start.24 = (s32[128]{0:T(128)S(1)}, s32[128]{0:T(128)}, u32[]{:S(2)}) copy-start(s32[128]{0:T(128)} %copy-done.23) | copy-start | bytes 1540
  158.9 13.2 %copy-start.34 = (bf16[384]{0:T(512)(128)(2,1)S(1)}, bf16[384]{0:T(512)(128)(2,1)}, u32[]{:S(2)}) copy-start(bf16[384]{0:T(512)(128)(2,1)} %param.34) | copy-start | bytes 2308
  158.9 13.3 %copy-start.14 = (bf16[192,384]{1,0:T(8,128)(2,1)S(1)}, bf16[192,384]{1,0:T(8,128)(2,1)}, u32[]{:S(2)}) copy-start(bf16[192,384]{1,0:T(8,128)(2,1)} %param.24) | copy-start | bytes 442372
  158.9 13.3 %copy-start.26 = (s32[192]{0:T(256)S(1)}, s32[192]{0:T(256)}, u32[]{:S(2)}) copy-start(s32[192]{0:T(256)} %copy-done.25) | copy-start | bytes 2308
  158.9 13.3 %copy-start.31 = (pred[192]{0:T(512)(128)(4,1)S(1)}, pred[192]{0:T(512)(128)(4,1)}, u32[]{:S(2)}) copy-start(pred[192]{0:T(512)(128)(4,1)} %get-tuple-element.60) | copy-start | bytes 580
  158.9 13.8 %copy-start.17 = (f32[2,12,384]{2,0,1:T(2,128)S(1)}, f32[2,12,384]{2,0,1:T(2,128)}, u32[]{:S(2)}) copy-start(f32[2,12,384]{2,0,1:T(2,128)} %param.35) | copy-start | bytes 110596
  159.1 13.7 %copy-start.4 = (bf16[2,384,3,6,64]{1,4,3,2,0:T(8,128)(2,1)S(1)}, bf16[2,384,3,6,64]{1,4,3,2,0:T(8,128)(2,1)}, u32[]{:S(2)}) copy-start(bf16[2,384,3,6,64]{1,4,3,2,0:T(8,128)(2,1)} %param.36) | copy-start | bytes 5308420
  259.3 25.7 %copy-start.12 = (bf16[2,6,64,384]{3,2,1,0:T(8,128)(2,1)S(1)}, bf16[2,6,64,384]{3,2,1,0:T(8,128)(2,1)}, u32[]{:S(2)}) copy-start(bf16[2,6,64,384]{3,2,1,0:T(8,128)(2,1)} %param.37) | copy-start | bytes 1769476
  405.2 5.2 %copy-start.30 = (f32[2,384]{1,0:T(2,128)S(1)}, f32[2,384]{1,0:T(2,128)}, u32[]{:S(2)}) copy-start(f32[2,384]{1,0:T(2,128)} %param.40) | copy-start | bytes 9220
  410.4 3.0 copy-start.1
  (4 other events, 4.4 us)

commit v3 on v0

v3 whole, which is shorter than its diff:
```python
import functools
import jax
import jax.numpy as jnp
from jax import lax
from jax.experimental import pallas as pl
from jax.experimental.pallas import tpu as pltpu
from jax.sharding import PartitionSpec as P

LN_EPS = 1e-6
TOKEN_AXES = ("batch", "time", "region")
SIDE = 4
REGIONS = SIDE ** 3
ROW = SIDE * 2
HEAD = 64
MESH = pl.DeviceIdType.MESH
NEAR = (1, SIDE - 1)
VMEM_LIMIT = 60 * 1024 * 1024
LOG2E = 1.4426950408889634
SAFE_SCORE = 60.0
SAFE_VALUE = 1e7


def position():
    t, r = lax.axis_index("time"), lax.axis_index("region")
    return t, r // 16, lax.rem(r // 4, 4), lax.rem(r, 4)


def device(t, z, y, x):
    return {"time": t, "region": z * 16 + y * 4 + x}


def turn(a, d):
    return lax.rem(a + d, SIDE)


def signal_all(peers):
    barrier = pltpu.get_barrier_semaphore()
    for peer in peers:
        pl.semaphore_signal(barrier, inc=1, device_id=device(*peer), device_id_type=MESH)
    pl.semaphore_wait(barrier, len(peers))


class Sender:
    def __init__(self, sems, place):
        self.sems, self.place, self.used, self.started = sems, place, 0, []

    def __call__(self, src, dst, recv_sem, peer):
        copy = remote_copy(src, dst, self.sems.at[self.used], recv_sem, peer)
        copy.start()
        self.used += 1
        self.started.append(copy)

    def arrived(self, ref, recv_sem):
        remote_copy(ref, ref, self.sems.at[0], recv_sem, self.place).wait_recv()

    def drain(self):
        for copy in self.started:
            copy.wait_send()


def remote_copy(src, dst, send_sem, recv_sem, peer):
    return pltpu.make_async_remote_copy(
        src_ref=src, dst_ref=dst, send_sem=send_sem, recv_sem=recv_sem, device_id=device(*peer), device_id_type=MESH
    )


def attend_kernel(heads, a_ref, b_ref, q_ref, part_ref, kva_ref, kvb_ref, qz_ref, guard_ref, qall_ref, acc_ref, stat_ref, vta_ref, vtb_ref, norm_ref, send_sem, one_recv, chunk_recv, q_recv):
    t, z, y, x = position()
    other = 1 - t
    near = [(0, other)] + [(d, c) for d in NEAR for c in range(2)]
    peers = [(other, z, y, x)]
    for d, c in near[1:]:
        peers += [(c, turn(z, d), y, x), (c, z, turn(y, d), x), (c, z, y, turn(x, d))]
    signal_all(peers)

    sources, chunks, turned_values = (a_ref, b_ref), (kva_ref, kvb_ref), (vta_ref, vtb_ref)
    lines, places = (z, y), (y, z)
    send = Sender(send_sem, (t, z, y, x))

    def along(half, first, d, c):
        return (c, z, turn(y, d), x) if (half == 0) == first else (c, turn(z, d), y, x)

    def block(half, place, c, size=1):
        at = chunks[half].at[lines[half]]
        return at.at[place * 2 + c] if size == 1 else at.at[pl.ds(place * 2, size)]

    def one(half, place, c):
        return one_recv.at[half, place * 2 + c]

    def onward(half, ref):
        for d in NEAR:
            send(ref, ref, chunk_recv.at[half, lines[half]], along(half, False, d, t))

    row = x * 2 + t
    for d, c in near:
        send(q_ref.at[c], qall_ref.at[row], q_recv.at[row], (c, z, y, turn(x, d)))
        for half in range(2):
            send(sources[half].at[c], block(half, places[half], t), one(half, places[half], t), along(half, True, d, c))
    for half in range(2):
        for d in NEAR:
            send(sources[half].at[t], block(half, places[half], t), chunk_recv.at[half, lines[half]], along(half, False, d, t))
        chunks[half][lines[half], places[half] * 2 + t] = sources[half][t]
    qall_ref[row] = q_ref[t]

    acc_ref[...] = jnp.zeros_like(acc_ref)
    stat_ref[...] = jnp.zeros_like(stat_ref)
    norm_ref[...] = jnp.zeros_like(norm_ref)
    qz_ref[...] = jnp.zeros_like(qz_ref)

    def q_arrived(d, c):
        at = turn(x, SIDE - d) * 2 + c
        send.arrived(qall_ref.at[at], q_recv.at[at])
        return at

    for d, relayed in zip(NEAR, range(2)):
        for c in range(2):
            at = q_arrived(d, c)
            if c == relayed:
                send(qall_ref.at[at], qall_ref.at[at], q_recv.at[at], (t, z, y, turn(x, d)))
        for half in range(2):
            place = turn(places[half], SIDE - d)
            for c in range(2):
                send.arrived(block(half, place, c), one(half, place, c))
            ref = block(half, place, relayed)
            send(ref, ref, one(half, place, relayed), along(half, True, d, t))
            onward(half, block(half, place, 0, 2))
    q_arrived(0, other)
    for half in range(2):
        ref = block(half, places[half], other)
        send.arrived(ref, one(half, places[half], other))
        onward(half, ref)
    for half in range(2):
        place = turn(places[half], 2)
        for c in range(2):
            send.arrived(block(half, place, c), one(half, place, c))
        onward(half, block(half, place, 0, 2))
    for c in range(2):
        q_arrived(2, c)

    rows = q_ref.shape[1]
    count = ROW * rows
    padded = qz_ref.shape[-1] * heads * HEAD // q_ref.shape[-1]
    lane = lax.broadcasted_iota(jnp.int32, (1, 128), 1)
    q_norm = jnp.zeros((1, 128), jnp.float32)
    for p in range(q_ref.shape[-1] // 128):
        flat = qall_ref[:, :, p * 128:(p + 1) * 128].reshape(count, 128)
        if padded > count:
            flat = jnp.concatenate([flat, jnp.zeros((padded - count, 128), flat.dtype)], axis=0)
        turned = flat.T
        for i in range(2):
            group, h = divmod(2 * p + i, heads)
            own = turned[i * HEAD:(i + 1) * HEAD]
            at = h % 2 * HEAD
            qz_ref[h, at:at + HEAD, group * padded:(group + 1) * padded] = own
            size = jnp.sum(own.astype(jnp.float32) ** 2, axis=0, keepdims=True)
            q_norm = jnp.where(lane == h, jnp.maximum(q_norm, jnp.max(size, axis=1, keepdims=True)), q_norm)

    width = heads * HEAD
    lanes = acc_ref.shape[-1]
    v_first = width // 128 * 128
    v_base = width - v_first
    pairs = -(-heads // 2) * 128
    picks = lax.broadcasted_iota(jnp.int32, (pairs, 128), 0) // HEAD == lax.broadcasted_iota(jnp.int32, (pairs, 128), 1)
    picks = (picks & (lane < heads)).astype(jnp.bfloat16)
    far = [len(send.started) + i for i in range(4)]

    def passed_on(half, i):
        d = NEAR[i]
        line = turn(lines[half], SIDE - d)
        ref = chunks[half].at[line, pl.ds(i * SIDE, SIDE)]
        return remote_copy(ref, ref, send_sem.at[far[2 * half + i]], chunk_recv.at[half, line], along(half, False, d, t))

    def chunk(j, _):
        ahead = j + j // 2 - 2 * (j // 3)

        @pl.when(j == 1)
        def near_chunks():
            for i in range(2):
                for half in range(2):
                    line = turn(lines[half], SIDE - NEAR[i])
                    send.arrived(chunks[half].at[line], chunk_recv.at[half, line])
                    passed_on(half, i).start()

        @pl.when(j == 3)
        def far_chunks():
            for half in range(2):
                line = turn(lines[half], 2)
                send.arrived(chunks[half].at[line], chunk_recv.at[half, line])

        for half in range(2):
            line = turn(lines[half], ahead)
            keys = ROW * sources[half].shape[1]
            vt_ref = turned_values[half]

            def load(first, last, half=half, line=line, keys=keys):
                return chunks[half][line, :, :, first:last].reshape(keys, last - first)

            values = load(v_first, v_first + vt_ref.shape[0])
            vt_ref[...] = values.T
            sizes = jnp.abs(values.astype(jnp.float32))
            for p in range(vt_ref.shape[0] // 128):
                part = sizes[:, p * 128:(p + 1) * 128].reshape(keys // 8, 8, 128)
                norm_ref[1] = jnp.maximum(norm_ref[1], jnp.max(part, axis=0))
            k_rows = load(0, pairs).astype(jnp.float32)
            sums = jnp.dot((k_rows * k_rows).astype(jnp.bfloat16), picks, preferred_element_type=jnp.float32)
            norm_ref[0] = jnp.maximum(norm_ref[0], jnp.max(sums.reshape(keys // 8, 8, 128), axis=0))

            def query_block(b, _, load=load, keys=keys, vt_ref=vt_ref):
                at = pl.multiple_of(b * lanes, lanes)
                for h in range(heads):
                    first = h // 2 * 128
                    scores = jnp.dot(load(first, first + 128), qz_ref[h, :, pl.ds(at, lanes)], preferred_element_type=jnp.float32)
                    weights = jnp.exp2(scores * (HEAD ** -0.5 * LOG2E))
                    stat_ref[b, h] += jnp.sum(weights.reshape(keys // 8, 8, lanes), axis=0)
                    values_t = vt_ref[v_base + h * HEAD:v_base + (h + 1) * HEAD]
                    acc_ref[b, h * HEAD:(h + 1) * HEAD] += jnp.dot(values_t, weights.astype(jnp.bfloat16), preferred_element_type=jnp.float32)
                return 0

            lax.fori_loop(0, acc_ref.shape[0], query_block, 0)
        return 0

    lax.fori_loop(0, SIDE, chunk, 0)
    total = part_ref.shape[0]
    for b in range(acc_ref.shape[0]):
        for h in range(heads):
            at = width + heads + h
            acc_ref[b, at:at + 1] = jnp.sum(stat_ref[b, h], axis=0, keepdims=True)
        last = min(total, (b + 1) * lanes)
        part_ref[b * lanes:last] = acc_ref[b].T[:last - b * lanes]
    guard_ref[0] = jnp.broadcast_to(jnp.max(norm_ref[0], axis=0, keepdims=True) * q_norm, (8, 128))
    guard_ref[1] = norm_ref[1]
    send.drain()
    for half in range(2):
        for i in range(2):
            passed_on(half, i).wait_send()


def mend_kernel(heads, guard_ref, part_in, kva_ref, kvb_ref, qz_ref, part_ref, a_ref, b_ref, q_ref, acc_ref, stat_ref, out_ref, sem):
    del part_in
    limit = (SAFE_SCORE * HEAD ** 0.5) ** 2 / 1.05
    safe = (jnp.max(guard_ref[0]) <= limit) & (jnp.max(guard_ref[1]) <= SAFE_VALUE)

    def fetch(src, dst):
        copy = pltpu.make_async_copy(src, dst, sem)
        copy.start()
        copy.wait()

    @pl.when(jnp.logical_not(safe))
    def again():
        width = heads * HEAD
        lanes = q_ref.shape[-1]
        total = out_ref.shape[0]

        def query_block(b, _):
            at = pl.multiple_of(b * lanes, lanes)
            fetch(qz_ref.at[:, :, pl.ds(at, lanes)], q_ref)
            acc_ref[...] = jnp.zeros_like(acc_ref)
            for h in range(heads):
                stat_ref[h] = jnp.full((8, lanes), -jnp.inf, jnp.float32)
                stat_ref[heads + h] = jnp.zeros((8, lanes), jnp.float32)
            for kv_ref, keys_ref in ((kva_ref, a_ref), (kvb_ref, b_ref)):

                def keys_block(i, _, kv_ref=kv_ref, keys_ref=keys_ref):
                    fetch(kv_ref.at[i // ROW, lax.rem(i, ROW)], keys_ref)
                    for h in range(heads):
                        first = h // 2 * 128
                        scores = jnp.dot(keys_ref[:, first:first + 128], q_ref[h], preferred_element_type=jnp.float32) * HEAD ** -0.5
                        old = stat_ref[h, 0:1]
                        new = jnp.maximum(old, jnp.max(scores, axis=0, keepdims=True))
                        weights = jnp.exp(scores - new)
                        fade = jnp.exp(old - new)
                        stat_ref[h, 0:1] = new
                        stat_ref[heads + h, 0:1] = stat_ref[heads + h, 0:1] * fade + jnp.sum(weights, axis=0, keepdims=True)
                        values = keys_ref[:, width + h * HEAD:width + (h + 1) * HEAD]
                        summed = lax.dot_general(values, weights.astype(jnp.bfloat16), (((0,), (0,)), ((), ())), preferred_element_type=jnp.float32)
                        acc_ref[h * HEAD:(h + 1) * HEAD] = acc_ref[h * HEAD:(h + 1) * HEAD] * fade + summed
                    return 0

                lax.fori_loop(0, SIDE * ROW, keys_block, 0)
            for h in range(heads):
                acc_ref[width + h:width + h + 1] = stat_ref[h, 0:1]
                acc_ref[width + heads + h:width + heads + h + 1] = stat_ref[heads + h, 0:1]
            out_ref[...] = acc_ref[...].T[:total]
            fetch(out_ref, part_ref.at[pl.ds(pl.multiple_of(b * total, 8), total)])
            return 0

        lax.fori_loop(0, part_ref.shape[0] // total, query_block, 0)


def attend(a, b, q, heads, collective_id):
    lanes = a.shape[-1]
    sets = q.shape[-1] // (heads * HEAD)
    count = ROW * q.shape[1] * sets
    block = 512 if count % 512 == 0 else 256
    blocks = -(-count // block)
    out_lanes = -(-(heads * HEAD + 2 * heads) // 128) * 128
    v_rows = lanes - heads * HEAD // 128 * 128
    vmem = pl.BlockSpec(memory_space=pltpu.VMEM)
    anywhere = pl.BlockSpec(memory_space=pl.ANY)
    part, kva, kvb, qz, guard = pl.pallas_call(
        functools.partial(attend_kernel, heads),
        out_shape=(
            jax.ShapeDtypeStruct((count, out_lanes), jnp.float32),
            jax.ShapeDtypeStruct((SIDE, ROW) + a.shape[1:], a.dtype),
            jax.ShapeDtypeStruct((SIDE, ROW) + b.shape[1:], b.dtype),
            jax.ShapeDtypeStruct((heads, 128, blocks * block), q.dtype),
            jax.ShapeDtypeStruct((2, 8, 128), jnp.float32),
        ),
        in_specs=[vmem] * 3,
        out_specs=(vmem,) * 5,
        scratch_shapes=[
            pltpu.VMEM((ROW,) + q.shape[1:], q.dtype),
            pltpu.VMEM((blocks, out_lanes, block), jnp.float32),
            pltpu.VMEM((blocks, heads, 8, block), jnp.float32),
            pltpu.VMEM((v_rows, ROW * a.shape[1]), jnp.bfloat16),
            pltpu.VMEM((v_rows, ROW * b.shape[1]), jnp.bfloat16),
            pltpu.VMEM((2, 8, 128), jnp.float32),
            pltpu.SemaphoreType.DMA((64,)),
            pltpu.SemaphoreType.DMA((2, ROW)),
            pltpu.SemaphoreType.DMA((2, SIDE)),
            pltpu.SemaphoreType.DMA((ROW,)),
        ],
        compiler_params=pltpu.CompilerParams(collective_id=collective_id, has_side_effects=True, vmem_limit_bytes=VMEM_LIMIT),
        name="attend",
    )(a, b, q)
    return pl.pallas_call(
        functools.partial(mend_kernel, heads),
        out_shape=jax.ShapeDtypeStruct(part.shape, part.dtype),
        in_specs=[vmem] + [anywhere] * 4,
        out_specs=anywhere,
        input_output_aliases={1: 0},
        scratch_shapes=[
            pltpu.VMEM(a.shape[1:], a.dtype),
            pltpu.VMEM(b.shape[1:], b.dtype),
            pltpu.VMEM((heads, 128, block), q.dtype),
            pltpu.VMEM((out_lanes, block), jnp.float32),
            pltpu.VMEM((2 * heads, 8, block), jnp.float32),
            pltpu.VMEM((min(count, block), out_lanes), jnp.float32),
            pltpu.SemaphoreType.DMA,
        ],
        compiler_params=pltpu.CompilerParams(vmem_limit_bytes=VMEM_LIMIT),
        name="mend",
    )(guard, part, kva, kvb, qz)


def combine_kernel(heads, part_ref, out_ref, got_ref, relay_ref, send_sem, recv_sem, relay_recv):
    t, z, y, x = position()
    sets, _, rows, _ = part_ref.shape
    near = [(0, 1 - t)] + [(d, c) for d in NEAR for c in range(2)]
    distant = [(2, c) for c in range(2)]
    if sets == 1:
        near += distant
    signal_all([(c, z, y, turn(x, d)) for d, c in near])
    send = Sender(send_sem, (t, z, y, x))
    mine = x * 2 + t
    if sets == 2:
        for _, c in distant:
            for s, d in enumerate(NEAR):
                send(part_ref.at[s, turn(x, 2) * 2 + c], relay_ref.at[s, t], relay_recv.at[s, t], (c, z, y, turn(x, d)))
    for d, c in near:
        for s in range(sets):
            send(part_ref.at[s, turn(x, d) * 2 + c], got_ref.at[s, mine], recv_sem.at[s, mine], (c, z, y, turn(x, d)))
    for s in range(sets):
        got_ref[s, mine] = part_ref[s, mine]
    if sets == 2:
        for c in range(2):
            for s, d in enumerate(NEAR):
                at = turn(x, SIDE - d) * 2 + c
                send.arrived(relay_ref.at[s, c], relay_recv.at[s, c])
                send(relay_ref.at[s, c], got_ref.at[s, at], recv_sem.at[s, at], (t, z, y, turn(x, d)))
    for d, c in near + (distant if sets == 2 else []):
        at = turn(x, SIDE - d) * 2 + c
        for s in range(sets):
            send.arrived(got_ref.at[s, at], recv_sem.at[s, at])
    width = heads * HEAD
    out_width = out_ref.shape[-1]
    head_of = lax.broadcasted_iota(jnp.int32, (rows, out_width), 1) // HEAD

    def spread(columns):
        full = jnp.broadcast_to(columns[:, 0:1], (rows, out_width))
        for h in range(1, heads):
            full = jnp.where(head_of == h, columns[:, h:h + 1], full)
        return full

    for c in range(2):
        for s in range(sets):
            blocks = [got_ref[s, 2 * i + c] for i in range(SIDE)]
            tops = [b[:, width:width + heads] for b in blocks]
            top = functools.reduce(jnp.maximum, tops)
            fades = [jnp.exp(m - top) for m in tops]
            total = sum(f * b[:, width + heads:width + 2 * heads] for f, b in zip(fades, blocks))
            merged = sum(spread(f / total) * b[:, :out_width] for f, b in zip(fades, blocks))
            out_ref[c, s] = jnp.where(head_of < heads, merged, 0.0).astype(jnp.bfloat16)
    send.drain()


def combine(parts, heads, collective_id):
    sets, _, rows, lanes = parts.shape
    out_width = -(-heads * HEAD // 128) * 128
    vmem = pl.BlockSpec(memory_space=pltpu.VMEM)
    out = pl.pallas_call(
        functools.partial(combine_kernel, heads),
        out_shape=jax.ShapeDtypeStruct((2, sets, rows, out_width), jnp.bfloat16),
        in_specs=[vmem],
        out_specs=vmem,
        scratch_shapes=[
            pltpu.VMEM(parts.shape, jnp.float32),
            pltpu.VMEM((2, 2, rows, lanes), jnp.float32),
            pltpu.SemaphoreType.DMA((24,)),
            pltpu.SemaphoreType.DMA((2, ROW)),
            pltpu.SemaphoreType.DMA((2, 2)),
        ],
        compiler_params=pltpu.CompilerParams(collective_id=collective_id, has_side_effects=True, vmem_limit_bytes=VMEM_LIMIT),
        name="combine",
    )(parts)
    return out.reshape(2, sets * rows, out_width)[:, :, :heads * HEAD]


def exchange_kernel(spread, src_ref, dst_ref, send_sem, recv_sem):
    t, me = lax.axis_index("time"), lax.axis_index("region")
    barrier = pltpu.get_barrier_semaphore()

    def signal(d, _):
        pl.semaphore_signal(barrier, inc=1, device_id={"time": t, "region": lax.rem(me + d, REGIONS)}, device_id_type=MESH)
        return 0

    lax.fori_loop(1, REGIONS, signal, 0)
    pl.semaphore_wait(barrier, REGIONS - 1)

    def start(d, _):
        peer = lax.rem(me + d, REGIONS)
        pltpu.make_async_remote_copy(
            src_ref=src_ref if spread else src_ref.at[peer],
            dst_ref=dst_ref.at[me],
            send_sem=send_sem,
            recv_sem=recv_sem,
            device_id={"time": t, "region": peer},
            device_id_type=MESH,
        ).start()
        return 0

    lax.fori_loop(1, REGIONS, start, 0)
    rest = dst_ref.at[pl.ds(0, REGIONS - 1)]
    everything = pltpu.make_async_remote_copy(
        src_ref=rest, dst_ref=rest, send_sem=send_sem, recv_sem=recv_sem, device_id={"time": t, "region": me}, device_id_type=MESH
    )
    everything.wait_recv()
    everything.wait_send()
    dst_ref[me] = src_ref[...] if spread else src_ref[me]


def exchange(rows, spread, collective_id):
    block = rows.shape if spread else rows.shape[1:]
    vmem = pl.BlockSpec(memory_space=pltpu.VMEM)
    return pl.pallas_call(
        functools.partial(exchange_kernel, spread),
        out_shape=jax.ShapeDtypeStruct((REGIONS,) + block, rows.dtype),
        in_specs=[vmem],
        out_specs=vmem,
        scratch_shapes=[pltpu.SemaphoreType.DMA, pltpu.SemaphoreType.DMA],
        compiler_params=pltpu.CompilerParams(collective_id=collective_id, has_side_effects=True),
        name="exchange",
    )(rows)


def layer_norm(hidden, ln_gain, ln_shift):
    hid_f32 = hidden.astype(jnp.float32)
    mean_val = jnp.mean(hid_f32, axis=-1, keepdims=True)
    centered = hid_f32 - mean_val
    variance = jnp.mean(centered * centered, axis=-1, keepdims=True)
    return centered * lax.rsqrt(variance + LN_EPS) * ln_gain + ln_shift


def run_block(hidden, vec_rows, w_qkv, w_o, w_one, w_two, collective_id):
    tokens, width = hidden.shape
    heads = w_qkv.shape[2] // 2
    half = heads * HEAD
    normed = layer_norm(hidden, vec_rows[0], vec_rows[1]).astype(jnp.bfloat16)
    w_rows = w_qkv.transpose(1, 2, 3, 0).reshape(3 * width, width)
    projected = lax.dot_general(normed, w_rows, (((1,), (1,)), ((), ())), preferred_element_type=jnp.float32)
    bias = jnp.concatenate([vec_rows[4], jnp.zeros_like(vec_rows[4]), vec_rows[5]])
    projected = (projected + bias).astype(jnp.bfloat16)

    def halves(part):
        return jnp.stack([projected[:, part * width + c * half:part * width + (c + 1) * half] for c in range(2)])

    q, k, v = halves(0), halves(1), halves(2)
    both = jnp.concatenate([k, v], axis=-1)
    split = tokens // 2 if tokens % 32 == 0 else 16
    sets = 2 if half % 128 else 1
    rows = tokens // sets
    q = jnp.concatenate([q[:, i * rows:(i + 1) * rows] for i in range(sets)], axis=-1)
    parts = attend(both[:, :split], both[:, split:], q, heads, collective_id)
    attended = combine(parts.reshape(sets, ROW, rows, -1), heads, collective_id + 1)
    w_o = w_o.reshape(2, half, width)
    mixed = sum(jnp.dot(attended[c], w_o[c], preferred_element_type=jnp.float32) for c in range(2))
    residual = (hidden.astype(jnp.float32) + mixed + vec_rows[6]).astype(jnp.bfloat16)
    normed_mlp = layer_norm(residual, vec_rows[2], vec_rows[3]).astype(jnp.bfloat16)
    mlp_hidden = jax.nn.gelu(jnp.dot(normed_mlp, w_one, preferred_element_type=jnp.float32) + vec_rows[8:12].reshape(-1), approximate=False).astype(jnp.bfloat16)
    return (residual.astype(jnp.float32) + jnp.dot(mlp_hidden, w_two, preferred_element_type=jnp.float32) + vec_rows[7]).astype(jnp.bfloat16)


def one_hot_rows(selector, rows):
    return jnp.dot(selector.astype(jnp.bfloat16), rows, preferred_element_type=jnp.float32).astype(jnp.bfloat16)


def solution(mesh):
    def local_step(patches, enc_pos, vis_mask, dec_pos, w_embed, b_embed, enc_vec, enc_wqkv, enc_wo, enc_w1, enc_w2, enc_final, w_dec_in, mask_token, dec_vec, dec_wqkv, dec_wo, dec_w1, dec_w2, dec_final, w_out):
        tokens = patches.shape[0]
        per_dev = tokens // 8
        me = lax.axis_index("region")
        own_count = jnp.sum(vis_mask)
        counts = exchange(jnp.full((8, 128), own_count, jnp.int32), True, 1)[:, 0, 0]
        embedded = (jnp.dot(patches, w_embed, preferred_element_type=jnp.float32) + b_embed + enc_pos.astype(jnp.float32)).astype(jnp.bfloat16)

        region_ids = jnp.arange(REGIONS, dtype=jnp.int32)
        starts = jnp.sum(jnp.where(region_ids[None, :] < region_ids[:, None], counts[None, :], 0), axis=1)
        start = jnp.sum(jnp.where(region_ids < me, counts, 0))
        token_ids = jnp.arange(tokens, dtype=jnp.int32)
        local_rank = jnp.sum(jnp.where(token_ids[None, :] < token_ids[:, None], vis_mask[None, :], 0), axis=1)
        send_row = jnp.where(vis_mask == 1, lax.rem(start + local_rank, REGIONS) * 2 + local_rank // REGIONS, -1)
        row_ids = jnp.arange(2 * REGIONS, dtype=jnp.int32)
        deal = row_ids[:, None] == send_row[None, :]
        source_starts, source_counts = jnp.repeat(starts, 2), jnp.repeat(counts, 2)
        rank = lax.rem(me - lax.rem(source_starts, REGIONS) + REGIONS, REGIONS) + REGIONS * lax.rem(row_ids, 2)
        place = jnp.where(rank < source_counts, (source_starts + rank) // REGIONS, -1)
        pack = jnp.arange(per_dev, dtype=jnp.int32)[:, None] == place[None, :]

        sent = one_hot_rows(deal, embedded).reshape(REGIONS, 2, -1)
        hidden = one_hot_rows(pack, exchange(sent, False, 2).reshape(2 * REGIONS, -1))
        for layer in range(enc_vec.shape[0]):
            hidden = run_block(hidden, enc_vec[layer], enc_wqkv[layer], enc_wo[layer], enc_w1[layer], enc_w2[layer], 4 + 2 * layer)
        latent = jnp.dot(layer_norm(hidden, enc_final[0], enc_final[1]).astype(jnp.bfloat16), w_dec_in, preferred_element_type=jnp.float32).astype(jnp.bfloat16)
        back = one_hot_rows(pack.T, latent).reshape(REGIONS, 2, -1)
        returned = exchange(back, False, 3).reshape(2 * REGIONS, -1)
        placed = jnp.dot(deal.T.astype(jnp.bfloat16), returned, preferred_element_type=jnp.float32)
        hidden = (jnp.where(vis_mask[:, None] == 1, placed, mask_token.astype(jnp.float32)) + dec_pos.astype(jnp.float32)).astype(jnp.bfloat16)
        for layer in range(dec_vec.shape[0]):
            hidden = run_block(hidden, dec_vec[layer], dec_wqkv[layer], dec_wo[layer], dec_w1[layer], dec_w2[layer], 8 + 2 * layer)
        return jnp.dot(layer_norm(hidden, dec_final[0], dec_final[1]).astype(jnp.bfloat16), w_out, preferred_element_type=jnp.float32)

    token_rows = P(TOKEN_AXES, None)
    token_flags = P(TOKEN_AXES)
    replicated = P()
    in_specs = (token_rows, token_rows, token_flags, token_rows) + (replicated,) * 17
    return jax.shard_map(local_step, mesh=mesh, in_specs=in_specs, out_specs=token_rows, check_vma=False)
```

time: 1210 us -> 355 us (0.29)
  waiting for transfers between devices: 608 us -> 0 us
  Pallas kernels: 0 us -> 275 us
  matrix products: 243 us -> 37.9 us
  local copies, waits for them, and re-layouts: 218 us -> 21.2 us
  other arithmetic: 78.2 us -> 13.8 us
  blocking collectives: 20.9 us -> 0 us
  between operations: 16.4 us -> 1.11 us
  starting transfers between devices: 12.8 us -> 0 us
    all_gather x8 -> x0, waiting for transfers between devices: 562 us -> none  [the longest x4 411 us: run_block(): key_rows = gather_rows(qkv_rows[:, 1])]
    pallas_call x0 -> x15, Pallas kernels: none -> 275 us  [the longest x4 157 us: attend(): pl.pallas_call(functools.partial(attend_kernel, heads), out_shape=(jax.Sh...]
    all_gather x4 -> x0, local copies, waits for them, and re-layouts: 195 us -> none  [the longest x2 97.5 us: run_block(): key_rows = gather_rows(qkv_rows[:, 1])]
    dot_general x14 -> x16, matrix products: 201 us -> 12.3 us  [the longest x8 5.19 us: run_block(): jnp.dot(attended[c], w_o[c], preferred_element_type=jnp.float32)]
    reduce_sum x4 -> x3, other arithmetic: 70.2 us -> 1.53 us  [the longest x1 0.78 us: local_step(): jnp.sum(jnp.where(token_ids[None, :] < token_ids[:, None], vis_mask[None,...]
    all_to_all x2 -> x0, waiting for transfers between devices: 45.3 us -> none  [the longest x1 30.3 us: local_step(): received = lax.all_to_all(send_rows, 'region', 0, 0, tiled=True)]
    unnamed x1 -> x0, blocking collectives: 20.9 us -> none
    sub x2 -> x0, matrix products: 16.4 us -> none  [attend(): attn_probs = jax.nn.softmax(scores, axis=-1).astype(jnp.bfloat16)]
  transfers between devices with their start and end apart: 10 -> 0, of which waited for: 10 -> 0; matrix products, arithmetic and copies ran while one was open for 24% -> 0% of each run, Pallas kernels for 0% -> 0%
where the time goes in v3:
time: 355 us; the launch traced here: 349 us
  Pallas kernels  275 us (77%)
  matrix products  37.9 us (11%)
  local copies, waits for them, and re-layouts  21.2 us (6%)
  other arithmetic  13.8 us (4%)
    pallas_call x4, Pallas kernels, attend(): pl.pallas_call(functools.partial(attend_kernel, heads), out_shape=(jax.Sh...  157 us
    pallas_call x4, Pallas kernels, combine(): pl.pallas_call(functools.partial(combine_kernel, heads), out_shape=jax.Sh...  74.5 us
    pallas_call x3, Pallas kernels, exchange(): pl.pallas_call(functools.partial(exchange_kernel, spread), out_shape=jax....  38.6 us
    dot_general x4, matrix products, run_block(): jnp.dot(mlp_hidden, w_two, preferred_element_type=jnp.float32)  22.7 us

profile of v3, /device:TPU:1, one launch (start us, length us, event | category | flops | bytes accessed | tf_op | source)
XLA Modules:
  0.0 349.0 jit_solution(5278978795279642980)
XLA Ops:
  0.0 1.8 slice_reduce_fusion.7
  2.4 1.3 reduce_sum.216
  3.7 1.2 broadcast_in_dim.47.src_ref
  4.9 15.5 %exchange.3 = s32[64,8,128]{2,1,0:T(8,128)} custom-call(s32[8,128]{1,0:T(8,128)} %broadcast_in_dim.47.src_ref), custom_call_target="tpu_custom_call" | custom-call | tf_op jit(solution)/shard_map/exchange/pallas_call | solution.py:455
  20.3 2.2 slice_reduce_fusion
  24.6 1.9 fusion.372
  26.4 2.0 convolution_convert_fusion
  29.2 11.7 %exchange.4 = bf16[64,2,768]{2,1,0:T(2,128)(2,1)} custom-call(bf16[64,2,768]{2,1,0:T(2,128)(2,1)} %reshape.337.src_ref), custom_call_target="tpu_custom_call" | custom-call | tf_op jit(solution)/shard_map/exchange/pallas_call | solution.py:455
  42.5 3.6 %fusion.499 = (bf16[1,768,3,12,64]{1,4,3,2,0:T(8,128)(2,1)S(1)}, bf16[1,768,3,12,64]{1,4,3,2,0:T(8,128)(2,1)S(1)}) fusion(bf16[2,768,3,12,64]{1,4,3,2,0:T(8,128)(2,1)} %param.28), kind=kLoop, calls=%fused_computation.627 | loop fusion | bytes 14155776 | tf_op jit(solution)/shard_map/slice | solution.py:532
  46.1 1.1 fusion.18
  49.0 23.2 %attend.4 = (f32[192,512]{1,0:T(8,128)}, bf16[4,8,16,768]{3,2,1,0:T(8,128)(2,1)}, bf16[4,8,8,768]{3,2,1,0:T(8,128)(2,1)}, bf16[6,128,256]{2,1,0:T(8,128)(2,1)}, f32[2,8,128]{2,1,0:T(8,128)}) custom-call(bf16[2,16,768]{2,1,0:T(8,128)(2,1)} %slice.530.a_ref, bf16[2,8,768]{2,1,0:T(8,128)(2,1)} %maximum_maximum_fusion.5.b_ref, ...), custom_call_target="tpu_custom_call" | custom-call | tf_op jit(solution)/shard_map/attend/pallas_call | solution.py:300
  72.3 1.4 mend.4
  73.6 13.1 %combine.4 = bf16[2,1,24,384]{3,2,1,0:T(8,128)(2,1)} custom-call(f32[1,8,24,512]{3,2,1,0:T(8,128)} %bitcast.236), custom_call_target="tpu_custom_call" | custom-call | tf_op jit(solution)/shard_map/combine/pallas_call | solution.py:401
  86.8 2.8 fusion.500
  91.5 1.4 fusion.505
  92.9 7.0 %fusion.508 = (f32[24]{0:T(128)}, f32[24,768]{1,0:T(8,128)}) fusion(f32[768]{0:T(1024)} %get-tuple-element.52, f32[24,768]{1,0:T(8,128)} %copy-done.9, bf16[2,3072,768]{2,1,0:T(8,128)(2,1)} %param.31, bf16[2,768,3072]{2,1,0:T(8,128)(2,1)} %param.30, f32[3072]{0:T(1024)} %bitcast.247, f32[768]{0:T(1024)} %get-tuple-element.53, f32[768]{0:T(1024)} %get-tuple-element.54, ...), kind=kOutput, calls=%fused_computation.636 | convolution fusion | flops 231542752 | bytes 9684064 | tf_op jit(solution)/shard_map/dot_general | solution.py:500
  101.7 2.0 fusion.19
  105.6 20.8 %attend.5 = (f32[192,512]{1,0:T(8,128)}, bf16[4,8,16,768]{3,2,1,0:T(8,128)(2,1)}, bf16[4,8,8,768]{3,2,1,0:T(8,128)(2,1)}, bf16[6,128,256]{2,1,0:T(8,128)(2,1)}, f32[2,8,128]{2,1,0:T(8,128)}) custom-call(bf16[2,16,768]{2,1,0:T(8,128)(2,1)} %slice.537.a_ref, bf16[2,8,768]{2,1,0:T(8,128)(2,1)} %maximum_maximum_fusion.4.b_ref, ...), custom_call_target="tpu_custom_call" | custom-call | tf_op jit(solution)/shard_map/attend/pallas_call | solution.py:300
  126.4 1.1 mend.5
  127.5 12.8 %combine.5 = bf16[2,1,24,384]{3,2,1,0:T(8,128)(2,1)} custom-call(f32[1,8,24,512]{3,2,1,0:T(8,128)} %bitcast.237), custom_call_target="tpu_custom_call" | custom-call | tf_op jit(solution)/shard_map/combine/pallas_call | solution.py:401
  142.6 5.8 %fusion.512 = (f32[24]{0:T(128)S(1)}, f32[24,768]{1,0:T(8,128)S(1)}) fusion(f32[768]{0:T(1024)S(1)} %copy-done.25, f32[24,768]{1,0:T(8,128)S(1)} %get-tuple-element.138, bf16[2,3072,768]{2,1,0:T(8,128)(2,1)} %param.31, bf16[2,768,3072]{2,1,0:T(8,128)(2,1)} %param.30, f32[3072]{0:T(1024)S(1)} %bitcast.246, f32[768]{0:T(1024)S(1)} %copy-done.24, ...), kind=kOutput, calls=%fused_computation.638 | convolution fusion | flops 231542752 | bytes 9684064 | tf_op jit(solution)/shard_map/dot_general | solution.py:500
  149.9 11.3 %exchange.5 = bf16[64,2,384]{2,1,0:T(2,128)(2,1)} custom-call(bf16[64,2,384]{2,1,0:T(2,128)(2,1)} %reshape.343.src_ref), custom_call_target="tpu_custom_call" | custom-call | tf_op jit(solution)/shard_map/exchange/pallas_call | solution.py:455
  164.8 56.3 %attend.6 = (f32[1536,256]{1,0:T(8,128)}, bf16[4,8,96,384]{3,2,1,0:T(8,128)(2,1)}, bf16[4,8,96,384]{3,2,1,0:T(8,128)(2,1)}, bf16[3,128,1536]{2,1,0:T(8,128)(2,1)}, f32[2,8,128]{2,1,0:T(8,128)}) custom-call(bf16[2,96,384]{2,1,0:T(8,128)(2,1)} %get-tuple-element.112.a_ref, bf16[2,96,384]{2,1,0:T(8,128)(2,1)} %get-tuple-element.111.b_ref, ...), custom_call_target="tpu_custom_call" | custom-call | tf_op jit(solution)/shard_map/attend/pallas_call | solution.py:300
  222.1 24.3 %combine.6 = bf16[2,2,96,256]{3,2,1,0:T(8,128)(2,1)} custom-call(f32[2,8,96,256]{3,2,1,0:T(8,128)} %bitcast.228), custom_call_target="tpu_custom_call" | custom-call | tf_op jit(solution)/shard_map/combine/pallas_call | solution.py:401
  248.2 4.9 %fusion.517 = (f32[192]{0:T(256)S(1)}, f32[192,384]{1,0:T(8,128)S(1)}) fusion(f32[384]{0:T(512)S(1)} %get-tuple-element.68, f32[192,384]{1,0:T(8,128)S(1)} %get-tuple-element.144, bf16[2,1536,384]{2,1,0:T(8,128)(2,1)} %param.39, bf16[2,384,1536]{2,1,0:T(8,128)(2,1)} %param.38, f32[1536]{0:T(1024)S(1)} %add.491, f32[384]{0:T(512)S(1)} %get-tuple-element.69, ...), kind=kOutput, calls=%fused_computation.641 | convolution fusion | flops 473186112 | bytes 3261184 | tf_op jit(solution)/shard_map/dot_general | solution.py:500
  255.6 57.0 %attend.7 = (f32[1536,256]{1,0:T(8,128)}, bf16[4,8,96,384]{3,2,1,0:T(8,128)(2,1)}, bf16[4,8,96,384]{3,2,1,0:T(8,128)(2,1)}, bf16[3,128,1536]{2,1,0:T(8,128)(2,1)}, f32[2,8,128]{2,1,0:T(8,128)}) custom-call(bf16[2,96,384]{2,1,0:T(8,128)(2,1)} %get-tuple-element.110.a_ref, bf16[2,96,384]{2,1,0:T(8,128)(2,1)} %get-tuple-element.109.b_ref, ...), custom_call_target="tpu_custom_call" | custom-call | tf_op jit(solution)/shard_map/attend/pallas_call | solution.py:300
  312.6 1.1 mend.7
  313.7 24.3 %combine.7 = bf16[2,2,96,256]{3,2,1,0:T(8,128)(2,1)} custom-call(f32[2,8,96,256]{3,2,1,0:T(8,128)} %bitcast.229), custom_call_target="tpu_custom_call" | custom-call | tf_op jit(solution)/shard_map/combine/pallas_call | solution.py:401
  338.0 1.1 fusion.317
  339.1 1.2 fusion.520
  340.5 4.9 %fusion.521 = (f32[192]{0:T(256)S(1)}, f32[192,384]{1,0:T(8,128)S(1)}) fusion(f32[384]{0:T(512)S(1)} %get-tuple-element.76, f32[192,384]{1,0:T(8,128)S(1)} %get-tuple-element.148, bf16[2,1536,384]{2,1,0:T(8,128)(2,1)} %param.39, bf16[2,384,1536]{2,1,0:T(8,128)(2,1)} %param.38, f32[1536]{0:T(1024)S(1)} %add.513, f32[384]{0:T(512)S(1)} %get-tuple-element.62, ...), kind=kOutput, calls=%fused_computation.643 | convolution fusion | flops 473186112 | bytes 3261184 | tf_op jit(solution)/shard_map/dot_general | solution.py:500
  345.7 3.0 fusion.222
  (146 shorter events, 24.9 us)
Async XLA Ops:
  0.0 26.4 %copy-start = (bf16[1536,768]{1,0:T(8,128)(2,1)S(1)}, bf16[1536,768]{1,0:T(8,128)(2,1)}, u32[]{:S(2)}) copy-start(bf16[1536,768]{1,0:T(8,128)(2,1)} %param.25) | copy-start | bytes 7077892
  23.1 18.8 %copy-start.19 = (s32[128]{0:T(128)}, s32[128]{0:T(128)S(1)}, u32[]{:S(2)}) copy-start(s32[128]{0:T(128)S(1)} %compare_select_fusion.6) | copy-start | bytes 1540
  26.4 2.0 copy-start.21
  42.4 3.6 %copy-start.12 = (f32[2304]{0:T(1024)S(1)}, f32[2304]{0:T(1024)}, u32[]{:S(2)}) copy-start(f32[2304]{0:T(1024)} %get-tuple-element.128) | copy-start | bytes 27652
  42.4 3.6 %copy-start.15 = (f32[768]{0:T(1024)S(1)}, f32[768]{0:T(1024)}, u32[]{:S(2)}) copy-start(f32[768]{0:T(1024)} %get-tuple-element.58) | copy-start | bytes 9220
  42.4 3.6 %copy-start.16 = (f32[768]{0:T(1024)S(1)}, f32[768]{0:T(1024)}, u32[]{:S(2)}) copy-start(f32[768]{0:T(1024)} %get-tuple-element.59) | copy-start | bytes 9220
  86.7 2.8 copy-start.11
  86.8 3.0 copy-start.14
  90.1 0.6 copy-start.9
  90.1 0.8 copy-start.29
  126.3 14.0 %copy-start.3 = (bf16[1,6,64,768]{3,2,1,0:T(8,128)(2,1)S(1)}, bf16[1,6,64,768]{3,2,1,0:T(8,128)(2,1)}, u32[]{:S(2)}) copy-start(bf16[1,6,64,768]{3,2,1,0:T(8,128)(2,1)} %get-tuple-element.90) | copy-start | bytes 1769476
  126.3 14.9 %copy-start.2 = (bf16[1,6,64,768]{3,2,1,0:T(8,128)(2,1)S(1)}, bf16[1,6,64,768]{3,2,1,0:T(8,128)(2,1)}, u32[]{:S(2)}) copy-start(bf16[1,6,64,768]{3,2,1,0:T(8,128)(2,1)} %get-tuple-element.87) | copy-start | bytes 1769476
  126.4 14.9 %copy-start.6 = (f32[24,768]{1,0:T(8,128)S(1)}, f32[24,768]{1,0:T(8,128)}, u32[]{:S(2)}) copy-start(f32[24,768]{1,0:T(8,128)} %get-tuple-element.136) | copy-start | bytes 221188
  127.5 15.0 %copy-start.17 = (f32[1,4,768]{2,0,1:T(1,128)S(1)}, f32[1,4,768]{2,0,1:T(1,128)}, u32[]{:S(2)}) copy-start(f32[1,4,768]{2,0,1:T(1,128)} %get-tuple-element.125) | copy-start | bytes 36868
  127.5 15.0 %copy-start.23 = (f32[768]{0:T(1024)S(1)}, f32[768]{0:T(1024)}, u32[]{:S(2)}) copy-start(f32[768]{0:T(1024)} %get-tuple-element.45) | copy-start | bytes 9220
  127.5 15.0 %copy-start.24 = (f32[768]{0:T(1024)S(1)}, f32[768]{0:T(1024)}, u32[]{:S(2)}) copy-start(f32[768]{0:T(1024)} %get-tuple-element.46) | copy-start | bytes 9220
  127.5 15.0 %copy-start.25 = (f32[768]{0:T(1024)S(1)}, f32[768]{0:T(1024)}, u32[]{:S(2)}) copy-start(f32[768]{0:T(1024)} %get-tuple-element.60) | copy-start | bytes 9220
  142.6 6.1 %copy-start.18 = (f32[2,768]{1,0:T(2,128)S(1)}, f32[2,768]{1,0:T(2,128)}, u32[]{:S(2)}) copy-start(f32[2,768]{1,0:T(2,128)} %param.32) | copy-start | bytes 18436
  142.6 6.2 %copy-start.7 = (bf16[768,384]{1,0:T(8,128)(2,1)S(1)}, bf16[768,384]{1,0:T(8,128)(2,1)}, u32[]{:S(2)}) copy-start(bf16[768,384]{1,0:T(8,128)(2,1)} %param.33) | copy-start | bytes 1769476
  142.6 6.2 %copy-start.20 = (s32[128]{0:T(128)S(1)}, s32[128]{0:T(128)}, u32[]{:S(2)}) copy-start(s32[128]{0:T(128)} %copy-done.19) | copy-start | bytes 1540
  148.4 13.8 %copy-start.28 = (bf16[384]{0:T(512)(128)(2,1)S(1)}, bf16[384]{0:T(512)(128)(2,1)}, u32[]{:S(2)}) copy-start(bf16[384]{0:T(512)(128)(2,1)} %param.34) | copy-start | bytes 2308
  148.4 13.8 %copy-start.10 = (bf16[192,384]{1,0:T(8,128)(2,1)S(1)}, bf16[192,384]{1,0:T(8,128)(2,1)}, u32[]{:S(2)}) copy-start(bf16[192,384]{1,0:T(8,128)(2,1)} %param.24) | copy-start | bytes 442372
  148.5 13.8 %copy-start.22 = (s32[192]{0:T(256)S(1)}, s32[192]{0:T(256)}, u32[]{:S(2)}) copy-start(s32[192]{0:T(256)} %copy-done.21) | copy-start | bytes 2308
  148.5 13.8 %copy-start.27 = (pred[192]{0:T(512)(128)(4,1)S(1)}, pred[192]{0:T(512)(128)(4,1)}, u32[]{:S(2)}) copy-start(pred[192]{0:T(512)(128)(4,1)} %get-tuple-element.84) | copy-start | bytes 580
  148.5 14.3 %copy-start.13 = (f32[2,12,384]{2,0,1:T(2,128)S(1)}, f32[2,12,384]{2,0,1:T(2,128)}, u32[]{:S(2)}) copy-start(f32[2,12,384]{2,0,1:T(2,128)} %param.35) | copy-start | bytes 110596
  148.7 14.2 %copy-start.4 = (bf16[2,384,3,6,64]{1,4,3,2,0:T(8,128)(2,1)S(1)}, bf16[2,384,3,6,64]{1,4,3,2,0:T(8,128)(2,1)}, u32[]{:S(2)}) copy-start(bf16[2,384,3,6,64]{1,4,3,2,0:T(8,128)(2,1)} %param.36) | copy-start | bytes 5308420
  222.1 24.3 %copy-start.8 = (bf16[2,6,64,384]{3,2,1,0:T(8,128)(2,1)S(1)}, bf16[2,6,64,384]{3,2,1,0:T(8,128)(2,1)}, u32[]{:S(2)}) copy-start(bf16[2,6,64,384]{3,2,1,0:T(8,128)(2,1)} %param.37) | copy-start | bytes 1769476
  246.5 0.9 copy-start.5
  340.5 5.2 %copy-start.26 = (f32[2,384]{1,0:T(2,128)S(1)}, f32[2,384]{1,0:T(2,128)}, u32[]{:S(2)}) copy-start(f32[2,384]{1,0:T(2,128)} %param.40) | copy-start | bytes 9220
  345.7 3.0 copy-start.1
